TPU v7x, 32 devices: a whole 2x2x4 slice. The times are simulated.
32 devices in a mesh: dp: 16 (over z, x, core), tensor: 2 (over y).
Axes of the slice: x: 2, y: 2, z: 4, core: 2. Of those that a mesh axis runs over, the one named last changes fastest.
Arguments:
- tokens: bfloat16 [32768, 768], P(('dp', 'tensor')), may hold values from -6 to 6
- seq_count: int32 [16], P('dp'), may hold values from 1 to 2, as said below
- first_gain: float32 [768], replicated, may hold values from 0.5 to 1.5
- first_shift: float32 [768], replicated, may hold values from -3 to 3
- heads_weight: bfloat16 [3, 768, 768], P(None, None, 'tensor'), may hold values from -0.21875 to 0.21875
- heads_bias: float32 [2, 768], P(None, 'tensor'), may hold values from -3 to 3
- mixing_weight: bfloat16 [768, 768], P('tensor'), may hold values from -1.75 to 1.75
- mixing_bias: float32 [768], replicated, may hold values from -3 to 3
- second_gain: float32 [768], replicated, may hold values from 0.5 to 1.5
- second_shift: float32 [768], replicated, may hold values from -3 to 3
- up_weight: bfloat16 [768, 3072], P(None, 'tensor'), may hold values from -0.21875 to 0.21875
- up_bias: float32 [3072], P('tensor'), may hold values from -3 to 3
- down_weight: bfloat16 [3072, 768], P('tensor'), may hold values from -0.3125 to 0.3125
- down_bias: float32 [768], replicated, may hold values from -3 to 3
- cotangent: bfloat16 [32768, 768], P(('dp', 'tensor')), may hold values from -6 to 6
Outputs:
- result: bfloat16 [32768, 768], P(('dp', 'tensor'))
- grad_tokens: bfloat16 [32768, 768], P(('dp', 'tensor'))
- grad_first_gain: float32 [768], replicated
- grad_first_shift: float32 [768], replicated
- grad_heads: float32 [3, 768, 768], P(None, None, 'tensor')
- grad_heads_bias: float32 [2, 768], P(None, 'tensor')
- grad_mixing: float32 [768, 768], P('tensor')
- grad_mixing_bias: float32 [768], replicated
- grad_second_gain: float32 [768], replicated
- grad_second_shift: float32 [768], replicated
- grad_up: float32 [768, 3072], P(None, 'tensor')
- grad_up_bias: float32 [3072], P('tensor')
- grad_down: float32 [3072, 768], P('tensor')
- grad_down_bias: float32 [768], replicated
Inputs may be any that keep to these rules, and one draw needn't show every extreme that they name: Data group g holds seq_count[g] sequences of 2048 / seq_count[g] tokens each, one after the other; both values occur in every draw.
All inputs are finite; a program needn't handle non-finite values.
Results may differ from a plain program's by a relative error of at most 0.015.
Values may be sent and summed in bfloat16 or wider, within the bound.
A program may use at most 320 MiB of HBM per device.

v0:
```python
import math

import jax
import jax.numpy as jnp
from jax import lax
from jax.sharding import PartitionSpec as P

HEAD = 64
DEPTH = 12


EPSILON = 1e-05
SCORE_SCALE = 0.125


def normalize_rows(values, gain, shift):
    centre = jnp.mean(values, axis=-1, keepdims=True)
    centred = values - centre
    spread = jnp.mean(centred * centred, axis=-1, keepdims=True)
    return centred * lax.rsqrt(spread + EPSILON) * gain + shift


def gelu_tanh(values):
    return (
        0.5
        * values
        * (
            1.0
            + jnp.tanh(math.sqrt(2.0 / math.pi) * (values + 0.044715 * values * values * values))
        )
    )


def seq_mask(first, count_rows, total, seq_total, key_rows):
    query_pos = first + lax.iota(jnp.int32, count_rows)
    key_pos = lax.iota(jnp.int32, key_rows)
    same = query_pos[:, None] * seq_total // total == key_pos[None, :] * seq_total // total
    return same & (key_pos[None, :] <= query_pos[:, None])


def local(
    tokens,
    seq_count,
    first_gain,
    first_shift,
    heads_weight,
    heads_bias,
    mixing_weight,
    mixing_bias,
    second_gain,
    second_shift,
    up_weight,
    up_bias,
    down_weight,
    down_bias,
    cotangent,
):
    branch = 1.0 / math.sqrt(DEPTH)
    seqs_here = seq_count[0]
    inputs = tokens.astype(jnp.float32)
    normed_one, undo_one = jax.vjp(normalize_rows, inputs, first_gain, first_shift)
    gathered_one = lax.all_gather(normed_one.astype(jnp.bfloat16), "tensor", axis=0, tiled=True)
    rows = gathered_one.shape[0]
    width = heads_weight.shape[2]
    heads = width // HEAD
    bias_rows = jnp.stack([heads_bias[0], jnp.zeros_like(heads_bias[0]), heads_bias[1]])
    projected = (
        jnp.einsum("rd,jde->jre", gathered_one, heads_weight, preferred_element_type=jnp.float32)
        + bias_rows[:, None, :]
    )
    projected = projected.astype(jnp.bfloat16)
    query = projected[0].reshape(rows, heads, HEAD)
    keys = projected[1].reshape(rows, heads, HEAD)
    values = projected[2].reshape(rows, heads, HEAD)
    block = min(512, rows)
    count_blocks = rows // block
    outputs_list = []
    logsum_list = []
    for index in range(count_blocks):
        start = index * block
        key_end = start + block
        scores = (
            jnp.einsum(
                "qhd,khd->hqk",
                query[start:key_end],
                keys[:key_end],
                preferred_element_type=jnp.float32,
            )
            * SCORE_SCALE
        )
        allowed = seq_mask(start, block, rows, seqs_here, key_end)
        scores = jnp.where(allowed[None], scores, -1e30)
        peak = jnp.max(scores, axis=-1, keepdims=True)
        expo = jnp.exp(scores - peak)
        total = jnp.sum(expo, axis=-1, keepdims=True)
        probs = (expo / total).astype(jnp.bfloat16)
        outputs_list.append(
            jnp.einsum("hqk,khd->qhd", probs, values[:key_end], preferred_element_type=jnp.float32)
        )
        logsum_list.append(peak + jnp.log(total))
    attended = jnp.concatenate(outputs_list, axis=0).reshape(rows, width).astype(jnp.bfloat16)
    attention_sum = lax.psum_scatter(
        jnp.dot(attended, mixing_weight, preferred_element_type=jnp.float32).astype(jnp.bfloat16),
        "tensor",
        scatter_dimension=0,
        tiled=True,
    ).astype(jnp.float32)
    middle = inputs + branch * (attention_sum + mixing_bias)
    normed_two, undo_two = jax.vjp(normalize_rows, middle, second_gain, second_shift)
    gathered_two = lax.all_gather(normed_two.astype(jnp.bfloat16), "tensor", axis=0, tiled=True)
    pre_act = jnp.dot(gathered_two, up_weight, preferred_element_type=jnp.float32) + up_bias
    activated, undo_gelu = jax.vjp(gelu_tanh, pre_act)
    act_low = activated.astype(jnp.bfloat16)
    mlp_sum = lax.psum_scatter(
        jnp.dot(act_low, down_weight, preferred_element_type=jnp.float32).astype(jnp.bfloat16),
        "tensor",
        scatter_dimension=0,
        tiled=True,
    ).astype(jnp.float32)
    result = (middle + branch * (mlp_sum + down_bias)).astype(jnp.bfloat16)
    grad_out = cotangent.astype(jnp.float32)
    grad_down_bias = branch * jnp.sum(grad_out, axis=0)
    grad_mlp = lax.all_gather(
        (branch * grad_out).astype(jnp.bfloat16), "tensor", axis=0, tiled=True
    )
    grad_down = jnp.einsum("rf,rd->fd", act_low, grad_mlp, preferred_element_type=jnp.float32)
    grad_act = jnp.einsum("rd,fd->rf", grad_mlp, down_weight, preferred_element_type=jnp.float32)
    grad_pre = undo_gelu(grad_act)[0].astype(jnp.bfloat16)
    grad_up_bias = jnp.sum(grad_pre, axis=0, dtype=jnp.float32)
    grad_up = jnp.einsum("rd,rf->df", gathered_two, grad_pre, preferred_element_type=jnp.float32)
    grad_normed_two = lax.psum_scatter(
        jnp.einsum("rf,df->rd", grad_pre, up_weight, preferred_element_type=jnp.float32).astype(
            jnp.bfloat16
        ),
        "tensor",
        scatter_dimension=0,
        tiled=True,
    ).astype(jnp.float32)
    grad_middle_norm, grad_second_gain, grad_second_shift = undo_two(grad_normed_two)
    grad_middle = grad_out + grad_middle_norm
    grad_mixing_bias = branch * jnp.sum(grad_middle, axis=0)
    grad_attn = lax.all_gather(
        (branch * grad_middle).astype(jnp.bfloat16), "tensor", axis=0, tiled=True
    )
    grad_mixing = jnp.einsum("re,rd->ed", attended, grad_attn, preferred_element_type=jnp.float32)
    grad_attended = jnp.einsum(
        "rd,ed->re", grad_attn, mixing_weight, preferred_element_type=jnp.float32
    )
    grad_attended = grad_attended.astype(jnp.bfloat16).reshape(rows, heads, HEAD)
    grad_keys = jnp.zeros((rows, heads, HEAD), jnp.float32)
    grad_values = jnp.zeros((rows, heads, HEAD), jnp.float32)
    grad_query_list = []
    for index in range(count_blocks):
        start = index * block
        key_end = start + block
        query_block = query[start:key_end]
        grad_block = grad_attended[start:key_end]
        scores = (
            jnp.einsum(
                "qhd,khd->hqk", query_block, keys[:key_end], preferred_element_type=jnp.float32
            )
            * SCORE_SCALE
        )
        allowed = seq_mask(start, block, rows, seqs_here, key_end)
        scores = jnp.where(allowed[None], scores, -1e30)
        probs_full = jnp.exp(scores - logsum_list[index])
        probs_low = probs_full.astype(jnp.bfloat16)
        grad_probs = jnp.einsum(
            "qhd,khd->hqk", grad_block, values[:key_end], preferred_element_type=jnp.float32
        )
        centre = jnp.sum(grad_probs * probs_full, axis=-1, keepdims=True)
        grad_scores = (probs_full * (grad_probs - centre)).astype(jnp.bfloat16)
        grad_query_list.append(
            jnp.einsum(
                "hqk,khd->qhd", grad_scores, keys[:key_end], preferred_element_type=jnp.float32
            )
            * SCORE_SCALE
        )
        grad_keys = grad_keys.at[:key_end].add(
            jnp.einsum("hqk,qhd->khd", grad_scores, query_block, preferred_element_type=jnp.float32)
            * SCORE_SCALE
        )
        grad_values = grad_values.at[:key_end].add(
            jnp.einsum("hqk,qhd->khd", probs_low, grad_block, preferred_element_type=jnp.float32)
        )
    grad_query = jnp.concatenate(grad_query_list, axis=0)
    grad_qkv = jnp.stack(
        [
            grad_query.reshape(rows, width),
            grad_keys.reshape(rows, width),
            grad_values.reshape(rows, width),
        ]
    ).astype(jnp.bfloat16)
    grad_heads_bias = jnp.stack(
        [
            jnp.sum(grad_qkv[0], axis=0, dtype=jnp.float32),
            jnp.sum(grad_qkv[2], axis=0, dtype=jnp.float32),
        ]
    )
    grad_heads = jnp.einsum(
        "rd,jre->jde", gathered_one, grad_qkv, preferred_element_type=jnp.float32
    )
    grad_normed_one = lax.psum_scatter(
        jnp.einsum(
            "jre,jde->rd", grad_qkv, heads_weight, preferred_element_type=jnp.float32
        ).astype(jnp.bfloat16),
        "tensor",
        scatter_dimension=0,
        tiled=True,
    ).astype(jnp.float32)
    grad_inputs_norm, grad_first_gain, grad_first_shift = undo_one(grad_normed_one)
    grad_tokens = (grad_middle + grad_inputs_norm).astype(jnp.bfloat16)
    grad_heads, grad_heads_bias, grad_mixing, grad_up, grad_up_bias, grad_down = lax.psum(
        (grad_heads, grad_heads_bias, grad_mixing, grad_up, grad_up_bias, grad_down), "dp"
    )
    small_grads = lax.psum(
        (
            grad_first_gain,
            grad_first_shift,
            grad_mixing_bias,
            grad_second_gain,
            grad_second_shift,
            grad_down_bias,
        ),
        ("dp", "tensor"),
    )
    groups = 1.0 / lax.axis_size("dp")
    small_grads = tuple((g * groups for g in small_grads))
    return (
        result,
        grad_tokens,
        small_grads[0],
        small_grads[1],
        grad_heads * groups,
        grad_heads_bias * groups,
        grad_mixing * groups,
        small_grads[2],
        small_grads[3],
        small_grads[4],
        grad_up * groups,
        grad_up_bias * groups,
        grad_down * groups,
        small_grads[5],
    )


def solution(mesh):
    placed = (
        P(("dp", "tensor"), None),
        P("dp"),
        P(),
        P(),
        P(None, None, "tensor"),
        P(None, "tensor"),
        P("tensor", None),
        P(),
        P(),
        P(),
        P(None, "tensor"),
        P("tensor"),
        P("tensor", None),
        P(),
        P(("dp", "tensor"), None),
    )
    return jax.shard_map(
        local,
        mesh=mesh,
        in_specs=placed,
        out_specs=(
            P(("dp", "tensor"), None),
            P(("dp", "tensor"), None),
            P(),
            P(),
            P(None, None, "tensor"),
            P(None, "tensor"),
            P("tensor", None),
            P(),
            P(),
            P(),
            P(None, "tensor"),
            P("tensor"),
            P("tensor", None),
            P(),
        ),
        check_vma=False,
    )
```

profile of v0, /device:TPU:0, one launch (start us, length us, event | category | flops | bytes accessed | tf_op | source)
XLA Modules:
  0.0 985.4 jit_solution(403022268459744688)
XLA Ops:
  20.3 41.6 %all-gather.5.cloned.1.call-done = bf16[2048,768]{1,0:T(8,128)(2,1)} async-done(((bf16[1024,768]{1,0:T(8,128)(2,1)}), bf16[2048,768]{1,0:T(8,128)(2,1)}) %all-gather.5.cloned.1.call-update) | async-done | bytes 3145744 | tf_op jit(solution)/shard_map/all_gather | solution.py:62
  116.3 10.9 %fusion.129 = (f32[6,512]{1,0:T(8,128)S(1)}, f32[6,512,2048]{2,1,0:T(8,128)}) fusion(bf16[512,6,64]{0,2,1:T(8,128)(2,1)S(1)} %bitcast.167, bf16[2048,6,64]{0,2,1:T(8,128)(2,1)S(1)} %bitcast.156, pred[512,2048]{1,0:T(8,128)(4,1)S(1)} %fusion.31), kind=kOutput, calls=%fused_computation.255 | convolution fusion | flops 824177664 | bytes 28192768 | tf_op jit(solution)/shard_map/qhd,khd->hqk/dot_general | solution.py:83
  127.2 10.5 %fusion = f32[6,512]{1,0:T(8,128)S(1)} fusion(f32[6,512,2048]{2,1,0:T(8,128)} %get-tuple-element.184, f32[6,512]{1,0:T(8,128)S(1)} %get-tuple-element.183), kind=kLoop, calls=%fused_computation.6 | loop fusion | flops 12579840 | bytes 25190400 | tf_op jit(solution)/shard_map/reduce_sum | solution.py:95
  137.8 11.0 %fusion.93 = bf16[512,6,64]{0,2,1:T(8,128)(2,1)S(1)} fusion(bf16[2048,6,64]{0,2,1:T(8,128)(2,1)S(1)} %bitcast.164, f32[6,512,2048]{2,1,0:T(8,128)} %get-tuple-element.184, f32[6,512]{1,0:T(8,128)S(1)} %fusion, f32[6,512]{1,0:T(8,128)S(1)} %get-tuple-element.183), kind=kOutput, calls=%fused_computation.151 | convolution fusion | flops 824377344 | bytes 27156480 | tf_op jit(solution)/shard_map/hqk,khd->qhd/dot_general | solution.py:98
  153.8 43.5 %reduce-scatter.5.cloned.1.call-done = bf16[1024,768]{1,0:T(8,128)(2,1)} async-done(((bf16[2048,768]{1,0:T(8,128)(2,1)}), bf16[1024,768]{1,0:T(8,128)(2,1)}) %reduce-scatter.5.cloned.1.call-update) | async-done | bytes 1572880 | tf_op jit(solution)/shard_map/reduce_scatter | solution.py:102
  206.3 42.1 %all-gather.7.cloned.1.call-done = bf16[2048,768]{1,0:T(8,128)(2,1)} async-done(((bf16[1024,768]{1,0:T(8,128)(2,1)}), bf16[2048,768]{1,0:T(8,128)(2,1)}) %all-gather.7.cloned.1.call-update) | async-done | bytes 3145744 | tf_op jit(solution)/shard_map/all_gather | solution.py:110
  248.4 13.6 %multiply_convert_fusion.3 = (bf16[2048,1536]{1,0:T(8,128)(2,1)}, f32[2048,1536]{1,0:T(8,128)}) fusion(f32[1536]{0:T(1024)S(1)} %copy-done.92, bf16[2048,768]{1,0:T(8,128)(2,1)} %all-gather.7.cloned.1.call-done, bf16[768,1536]{1,0:T(8,128)(2,1)S(1)} %copy-done), kind=kOutput, calls=%fused_computation.32 | convolution fusion | flops 4863295488 | bytes 24385536 | tf_op jit(solution)/shard_map/dot_general | solution.py:111
  262.1 33.3 %all-gather.9.cloned.1.call-done = bf16[2048,768]{1,0:T(8,128)(2,1)} async-done(((bf16[1024,768]{1,0:T(8,128)(2,1)}), bf16[2048,768]{1,0:T(8,128)(2,1)}) %all-gather.9.cloned.1.call-update) | async-done | bytes 3145744 | tf_op jit(solution)/shard_map/all_gather | solution.py:123
  295.3 19.4 %convert_reduce_fusion = (f32[1536]{0:T(1024)}, bf16[2048,1536]{1,0:T(8,128)(2,1)S(1)}) fusion(bf16[2048,768]{1,0:T(8,128)(2,1)} %all-gather.9.cloned.1.call-done, bf16[1536,768]{1,0:T(8,128)(2,1)} %param.47, f32[2048,1536]{1,0:T(8,128)} %get-tuple-element.192, f32[1536]{0:T(1024)S(1)} %copy-done.92), kind=kOutput, calls=%fused_computation.27 | convolution fusion | flops 4916771328 | bytes 24391680 | tf_op jit(solution)/shard_map/rd,fd->rf/dot_general | solution.py:127
  334.8 32.7 %reduce-scatter.9.cloned.1.call-done = bf16[1024,768]{1,0:T(8,128)(2,1)} async-done(((bf16[2048,768]{1,0:T(8,128)(2,1)}), bf16[1024,768]{1,0:T(8,128)(2,1)}) %reduce-scatter.9.cloned.1.call-update) | async-done | bytes 1572880 | tf_op jit(solution)/shard_map/reduce_scatter | solution.py:131
  371.5 42.0 %reduce-scatter.7.cloned.1.call-done = bf16[1024,768]{1,0:T(8,128)(2,1)} async-done(((bf16[2048,768]{1,0:T(8,128)(2,1)}), bf16[1024,768]{1,0:T(8,128)(2,1)}) %reduce-scatter.7.cloned.1.call-update) | async-done | bytes 1572880 | tf_op jit(solution)/shard_map/reduce_scatter | solution.py:114
  423.1 43.7 %all-gather.11.cloned.1.call-done = bf16[2048,768]{1,0:T(8,128)(2,1)} async-done(((bf16[1024,768]{1,0:T(8,128)(2,1)}), bf16[2048,768]{1,0:T(8,128)(2,1)}) %all-gather.11.cloned.1.call-update) | async-done | bytes 3145744 | tf_op jit(solution)/shard_map/all_gather | solution.py:142
  504.3 12.7 %multiply_reduce_fusion.1 = (f32[6,512]{1,0:T(8,128)}, f32[6,512,1536]{2,1,0:T(8,128)}) fusion(f32[6,512,1536]{2,1,0:T(8,128)} %get-tuple-element.186, f32[6,512]{1,0:T(8,128)S(1)} %copy-done.53, bf16[512,6,64]{0,2,1:T(8,128)(2,1)S(1)} %bitcast.177, bf16[1536,6,64]{0,2,1:T(8,128)(2,1)S(1)} %bitcast.170), kind=kOutput, calls=%fused_computation.11 | convolution fusion | flops 618132480 | bytes 39346176 | tf_op jit(solution)/shard_map/qhd,khd->hqk/dot_general | solution.py:168
  517.0 10.4 %fusion.65 = f32[2048,6,64]{0,2,1:T(8,128)} fusion(f32[2048,6,64]{0,2,1:T(8,128)} %fusion.73, bf16[512,6,64]{0,2,1:T(8,128)(2,1)S(1)} %bitcast.178, f32[6,512,1536]{2,1,0:T(8,128)} %get-tuple-element.186, f32[6,512]{1,0:T(8,128)S(1)} %copy-done.53), kind=kOutput, calls=%fused_computation.117 | convolution fusion | flops 614006784 | bytes 23998464 | tf_op jit(solution)/shard_map/hqk,qhd->khd/dot_general | solution.py:184
  527.5 20.2 %multiply_reduce_fusion = (f32[6,512]{1,0:T(8,128)}, f32[6,512,2048]{2,1,0:T(8,128)}) fusion(f32[6,512,2048]{2,1,0:T(8,128)} %get-tuple-element.184, f32[6,512]{1,0:T(8,128)S(1)} %log_add_fusion, bf16[512,6,64]{0,2,1:T(8,128)(2,1)S(1)} %bitcast.175, bf16[2048,6,64]{0,2,1:T(8,128)(2,1)S(1)} %bitcast.165), kind=kOutput, calls=%fused_computation.1 | convolution fusion | flops 824177664 | bytes 52322304 | tf_op jit(solution)/shard_map/qhd,khd->hqk/dot_general | solution.py:168
  547.7 11.5 %fusion.46 = bf16[2048,6,64]{0,2,1:T(8,128)(2,1)S(1)} fusion(f32[2048,6,64]{0,2,1:T(8,128)} %fusion.65, bf16[512,6,64]{0,2,1:T(8,128)(2,1)S(1)} %bitcast.176, f32[6,512,2048]{2,1,0:T(8,128)} %get-tuple-element.184, f32[6,512]{1,0:T(8,128)S(1)} %log_add_fusion), kind=kOutput, calls=%fused_computation.94 | convolution fusion | flops 819462144 | bytes 30289920 | tf_op jit(solution)/shard_map/hqk,qhd->khd/dot_general | solution.py:184
  561.3 9.6 multiply_convert_fusion.2
  576.1 18.0 %multiply_convert_fusion.1 = bf16[6,512,1536]{2,1,0:T(8,128)(2,1)} fusion(f32[6,512,1536]{2,1,0:T(8,128)} %get-tuple-element.198, f32[6,512,1536]{2,1,0:T(8,128)} %get-tuple-element.186, f32[6,512]{1,0:T(8,128)S(1)} %copy-done.64, f32[6,512]{1,0:T(8,128)S(1)} %copy-done.54), kind=kLoop, calls=%fused_computation.10 | loop fusion | flops 18874368 | bytes 47210496 | tf_op jit(solution)/shard_map/convert_element_type | solution.py:172
  609.3 15.1 %multiply_convert_fusion = bf16[6,512,2048]{2,1,0:T(8,128)(2,1)} fusion(f32[6,512,2048]{2,1,0:T(8,128)} %get-tuple-element.200, f32[6,512,2048]{2,1,0:T(8,128)S(1)} %bitcast.151, f32[6,512]{1,0:T(8,128)S(1)} %copy-done.65, f32[6,512]{1,0:T(8,128)S(1)} %log_add_fusion), kind=kLoop, calls=%fused_computation | loop fusion | flops 25165824 | bytes 62939136 | tf_op jit(solution)/shard_map/convert_element_type | solution.py:172
  624.5 9.4 fusion.90
  653.4 9.8 fusion.134
  685.1 63.6 %all-reduce.3 = (f32[2,384]{1,0:T(2,128)S(1)}, f32[1536]{0:T(1024)S(1)}) all-reduce(f32[2,384]{1,0:T(2,128)S(1)} %pad_maximum_fusion.6, f32[1536]{0:T(1024)S(1)} %copy-done.82), channel_id=1, replica_groups=mesh['dp'=16,'tensor'=2] {'dp'}, use_global_device_ids=true, to_apply=%region_31.32 | all-reduce | flops 2304 | bytes 18432 | tf_op jit(solution)/shard_map/psum | solution.py:213
  758.7 38.8 %all-reduce.2 = (f32[768]{0:T(1024)S(1)}, f32[768]{0:T(1024)S(1)}, f32[768]{0:T(1024)S(1)}, f32[768]{0:T(1024)S(1)}, f32[768]{0:T(1024)S(1)}, /*index=5*/f32[768]{0:T(1024)S(1)}) all-reduce(f32[768]{0:T(1024)S(1)} %get-tuple-element.142, f32[768]{0:T(1024)S(1)} %get-tuple-element.147, ...), channel_id=1, replica_groups=mesh['dp'=16,'tensor'=2] {'dp','tensor'}, use_global_device_ids=true, to_apply=%region_25.26 | all-reduce | flops 4608 | bytes 36864 | tf_op jit(solution)/shard_map/psum | solution.py:216
  801.0 159.2 %all-reduce.7.cloned.1.call-done = (f32[3,768,384]{1,2,0:T(8,128)}, f32[384,768]{1,0:T(8,128)}, f32[768,1536]{1,0:T(8,128)}, f32[1536,768]{1,0:T(8,128)}) async-done(((f32[3,768,384]{1,2,0:T(8,128)}, f32[384,768]{1,0:T(8,128)}, f32[768,1536]{1,0:T(8,128)}, f32[1536,768]{1,0:T(8,128)}), (f32[3,768,384]{1,2,0:T(8,128)}, f32[384,768]{1,0:T(8,128)}, f32[768,1536]{1,0:T(8,128)}, ...) | async-done | bytes 14155792 | tf_op jit(solution)/shard_map/psum | solution.py:213
  (339 shorter events, 246.7 us)
Async XLA Ops:
  7.2 241.2 %copy-start = (bf16[768,1536]{1,0:T(8,128)(2,1)S(1)}, bf16[768,1536]{1,0:T(8,128)(2,1)}, u32[]{:S(2)}) copy-start(bf16[768,1536]{1,0:T(8,128)(2,1)} %param.45) | copy-start | bytes 7077892
  7.2 54.7 %all-gather.5.cloned.1.call-start = ((), (), s32[]{:S(2)}) async-start(), calls=%async_computation.4 | async-start | bytes 4718592 | tf_op jit(solution)/shard_map/all_gather | solution.py:62
  14.2 183.2 %reduce-scatter.5.cloned.1.call-start = ((), (), s32[]{:S(2)}) async-start(), calls=%async_computation.5 | async-start | bytes 4718592 | tf_op jit(solution)/shard_map/reduce_scatter | solution.py:102
  153.7 43.6 %copy-start.63 = (f32[768]{0:T(1024)S(1)}, f32[768]{0:T(1024)}, u32[]{:S(2)}) copy-start(f32[768]{0:T(1024)} %param.42) | copy-start | bytes 9220
  153.8 47.4 %copy-start.79 = (f32[768]{0:T(1024)S(1)}, f32[768]{0:T(1024)}, u32[]{:S(2)}) copy-start(f32[768]{0:T(1024)} %param.43) | copy-start | bytes 9220
  153.8 47.4 %copy-start.85 = (f32[768]{0:T(1024)S(1)}, f32[768]{0:T(1024)}, u32[]{:S(2)}) copy-start(f32[768]{0:T(1024)} %param.44) | copy-start | bytes 9220
  153.8 94.6 %all-gather.7.cloned.1.call-start = ((), (), s32[]{:S(2)}) async-start(), calls=%async_computation.6 | async-start | bytes 4718592 | tf_op jit(solution)/shard_map/all_gather | solution.py:110
  203.3 45.1 %copy-start.92 = (f32[1536]{0:T(1024)S(1)}, f32[1536]{0:T(1024)}, u32[]{:S(2)}) copy-start(f32[1536]{0:T(1024)} %param.46) | copy-start | bytes 18436
  203.3 92.0 %all-gather.9.cloned.1.call-start = ((), (), s32[]{:S(2)}) async-start(), calls=%async_computation.8 | async-start | bytes 4718592 | tf_op jit(solution)/shard_map/all_gather | solution.py:123
  206.2 161.2 %reduce-scatter.9.cloned.1.call-start = ((), (), s32[]{:S(2)}) async-start(), calls=%async_computation.9 | async-start | bytes 4718592 | tf_op jit(solution)/shard_map/reduce_scatter | solution.py:131
  323.9 89.7 %reduce-scatter.7.cloned.1.call-start = ((), (), s32[]{:S(2)}) async-start(), calls=%async_computation.7 | async-start | bytes 4718592 | tf_op jit(solution)/shard_map/reduce_scatter | solution.py:114
  334.7 78.9 %copy-start.84 = (f32[768]{0:T(1024)S(1)}, f32[768]{0:T(1024)}, u32[]{:S(2)}) copy-start(f32[768]{0:T(1024)} %param.48) | copy-start | bytes 9220
  334.7 132.1 %all-gather.11.cloned.1.call-start = ((), (), s32[]{:S(2)}) async-start(), calls=%async_computation.10 | async-start | bytes 4718592 | tf_op jit(solution)/shard_map/all_gather | solution.py:142
  421.7 328.2 %reduce-scatter.11.cloned.1.call-start = ((), (), s32[]{:S(2)}) async-start(), calls=%async_computation.11 | async-start | bytes 4718592 | tf_op jit(solution)/shard_map/reduce_scatter | solution.py:203
  576.1 33.2 %slice-start = ((s8[25165824]{0:T(1024)(128)(4,1)}), s8[4194304]{0:T(1024)(128)(4,1)S(1)}, s32[]{:S(2)}) async-start(s8[25165824]{0:T(1024)(128)(4,1)} %bitcast.150), calls=%async_computation.13 | async-start | bytes 8388608
  576.1 33.2 %slice-start.1 = ((s8[25165824]{0:T(1024)(128)(4,1)}), s8[4194304]{0:T(1024)(128)(4,1)S(1)}, s32[]{:S(2)}) async-start(s8[25165824]{0:T(1024)(128)(4,1)} %bitcast.150), calls=%async_computation.14 | async-start | bytes 8388608
  576.1 33.2 %slice-start.2 = ((s8[25165824]{0:T(1024)(128)(4,1)}), s8[4194304]{0:T(1024)(128)(4,1)S(1)}, s32[]{:S(2)}) async-start(s8[25165824]{0:T(1024)(128)(4,1)} %bitcast.150), calls=%async_computation.15 | async-start | bytes 8388608
  576.1 33.2 %slice-start.3 = ((s8[25165824]{0:T(1024)(128)(4,1)}), s8[4194304]{0:T(1024)(128)(4,1)S(1)}, s32[]{:S(2)}) async-start(s8[25165824]{0:T(1024)(128)(4,1)} %bitcast.150), calls=%async_computation.16 | async-start | bytes 8388608
  653.3 306.9 %all-reduce.7.cloned.1.call-start = ((), (), s32[]{:S(2)}) async-start(), calls=%async_computation.12 | async-start | bytes 28311552 | tf_op jit(solution)/shard_map/psum | solution.py:213
  681.5 68.3 %copy-start.6 = (bf16[1024,768]{1,0:T(8,128)(2,1)S(1)}, bf16[1024,768]{1,0:T(8,128)(2,1)}, u32[]{:S(2)}) copy-start(bf16[1024,768]{1,0:T(8,128)(2,1)} %param.35) | copy-start | bytes 4718596
  681.6 68.3 %copy-start.58 = (f32[1024]{0:T(1024)S(1)}, f32[1024]{0:T(1024)}, u32[]{:S(2)}) copy-start(f32[1024]{0:T(1024)} %copy-done.57) | copy-start | bytes 12292
  681.6 68.3 %copy-start.68 = (f32[768]{0:T(1024)S(1)}, f32[768]{0:T(1024)}, u32[]{:S(2)}) copy-start(f32[768]{0:T(1024)} %param.37) | copy-start | bytes 9220
  681.6 71.0 %copy-start.76 = (f32[1024]{0:T(1024)S(1)}, f32[1024]{0:T(1024)}, u32[]{:S(2)}) copy-start(f32[1024]{0:T(1024)} %copy-done.75) | copy-start | bytes 12292
  681.6 71.0 %copy-start.70 = (f32[1024]{0:T(1024)S(1)}, f32[1024]{0:T(1024)}, u32[]{:S(2)}) copy-start(f32[1024]{0:T(1024)} %copy-done.69) | copy-start | bytes 12292
  (92 other events, 575.4 us)
Sparse Core Ops, SparseCore 0:
  14.3 47.6 all-gather.4
  153.9 43.3 reduce-scatter.4
  203.4 44.9 all-gather.6
  250.4 44.8 all-gather.8
  324.0 43.3 reduce-scatter.8
  370.1 43.4 reduce-scatter.6
  421.8 44.9 all-gather.10
  653.4 43.4 reduce-scatter.10
  702.6 257.5 all-reduce.6
where the time goes:
time: 996 us; the launch traced here: 985 us
  waiting for transfers between devices  438 us (44%)
  matrix products  261 us (26%)
  other arithmetic  134 us (13%)
  blocking collectives  102 us (10%)
  local copies, waits for them, and re-layouts  33.2 us (3%)
  between operations  16.1 us (2%)
    psum x1, waiting for transfers between devices, local(): lax.psum((grad_heads, grad_heads_bias, grad_mixing, grad_up, grad_up_bias...  159 us
    psum x1, blocking collectives, local(): lax.psum((grad_heads, grad_heads_bias, grad_mixing, grad_up, grad_up_bias...  63.6 us
    convert_element_type x4, other arithmetic, local(): grad_scores = (probs_full * (grad_probs - centre)).astype(jnp.bfloat16)  49.1 us
    dot_general x4, matrix products, local(): jnp.einsum('qhd,khd->hqk', grad_block, values[:key_end], preferred_elemen...  44 us
    all_gather x1, waiting for transfers between devices, local(): lax.all_gather((branch * grad_middle).astype(jnp.bfloat16), 'tensor', axi...  43.7 us
    reduce_scatter x1, waiting for transfers between devices, local(): lax.psum_scatter(jnp.dot(attended, mixing_weight, preferred_element_type=...  43.5 us
    all_gather x1, waiting for transfers between devices, local(): lax.all_gather(normed_two.astype(jnp.bfloat16), 'tensor', axis=0, tiled=T...  42.1 us
    reduce_scatter x1, waiting for transfers between devices, local(): lax.psum_scatter(jnp.dot(act_low, down_weight, preferred_element_type=jnp...  42 us
  transfers between devices with their start and end apart: 9, of which 8 were waited for; matrix products, arithmetic and copies ran while one was open for 8% of the time, Pallas kernels for 0%

commit v1 on v0

v1 whole, which is shorter than its diff:
```python
import functools, math
import jax
import jax.numpy as jnp
from jax import lax
from jax.experimental import pallas as pl
from jax.experimental.pallas import tpu as pltpu
from jax.sharding import PartitionSpec as P

HEAD = 64
LOG2E = math.log2(math.e)
NT = (((1,), (1,)), ((), ()))
TN = (((0,), (0,)), ((), ()))
f32 = jnp.float32
bf16 = jnp.bfloat16


def attn_forward_kernel(blk, info, own_ref, oth_ref, w_ref, b_ref, qkv_ref, att_ref, lse_ref, acc_ref, top_ref):
    qb = pl.program_id(0)
    nb = pl.num_programs(0)
    half = own_ref.shape[0]
    width = w_ref.shape[2]
    side, count = info[0], info[1]

    @pl.when(qb == 0)
    def _():
        step = 256
        for part, ref in enumerate((own_ref, oth_ref)):
            def rows_loop(i, _, part=part, ref=ref):
                rows = ref[pl.ds(pl.multiple_of(i * step, step), step), :]
                to = pl.multiple_of(part * half + i * step, step)
                for j in range(3):
                    y = jnp.dot(rows, w_ref[j], preferred_element_type=f32) + b_ref[pl.ds(j, 1), :]
                    y = y.astype(bf16)
                    if j == 0:
                        y = y * bf16(0.125)
                    qkv_ref[j, pl.ds(to, step), :] = y
                return 0
            lax.fori_loop(0, half // step, rows_loop, 0)

    def place(b):
        return pl.multiple_of(lax.rem(b + side * (nb // 2), nb) * blk, blk)

    lane_lo = lax.broadcasted_iota(jnp.int32, (blk, 128), 1) < HEAD
    first = (qb * count // nb) * nb // count
    q_at = place(qb)

    def block(kb, fresh, masked):
        k_at = place(kb)
        if masked:
            qi = lax.broadcasted_iota(jnp.int32, (blk, blk), 0)
            ki = lax.broadcasted_iota(jnp.int32, (blk, blk), 1)
            keep = ki <= qi
        for p in range(width // 128):
            cols = pl.ds(128 * p, 128)
            q = qkv_ref[0, pl.ds(q_at, blk), cols]
            k = qkv_ref[1, pl.ds(k_at, blk), cols]
            v = qkv_ref[2, pl.ds(k_at, blk), cols]
            for h in range(2):
                mine = lane_lo if h == 0 else ~lane_lo
                head = 2 * p + h
                qh = jnp.where(mine, q, bf16(0))
                vh = jnp.where(mine, v, bf16(1))
                s = lax.dot_general(qh, k, NT, preferred_element_type=f32) * LOG2E
                if masked:
                    s = jnp.where(keep, s, -1e30)
                top = jnp.max(s, axis=1, keepdims=True)
                if fresh:
                    e = jnp.exp2(s - top)
                    acc_ref[head] = jnp.dot(e.astype(bf16), vh, preferred_element_type=f32)
                    top_ref[head] = jnp.broadcast_to(top, (blk, 128))
                else:
                    old = top_ref[head]
                    new = jnp.maximum(old, top)
                    e = jnp.exp2(s - new[:, :1])
                    acc_ref[head] = acc_ref[head] * jnp.exp2(old - new) + jnp.dot(
                        e.astype(bf16), vh, preferred_element_type=f32)
                    top_ref[head] = new

    block(qb, True, True)

    def loop(kb, _):
        block(kb, False, False)
        return 0
    lax.fori_loop(first, qb, loop, 0)

    for p in range(width // 128):
        a0, a1 = acc_ref[2 * p], acc_ref[2 * p + 1]
        num = jnp.where(lane_lo, a0, a1)
        den = jnp.where(lane_lo, pltpu.roll(a0, HEAD, 1), pltpu.roll(a1, HEAD, 1))
        att_ref[pl.ds(q_at, blk), pl.ds(128 * p, 128)] = (num / den).astype(bf16)
        logs = jnp.where(lane_lo, top_ref[2 * p], top_ref[2 * p + 1]) + jnp.log2(den)
        rows = logs.T
        lse_ref[qb, pl.ds(2 * p, 1), :] = rows[0:1]
        lse_ref[qb, pl.ds(2 * p + 1, 1), :] = rows[HEAD:HEAD + 1]


def attn_forward(info, own, oth, w, b, blk=512):
    half = own.shape[0]
    rows = 2 * half
    width = w.shape[2]
    nb = rows // blk
    heads = width // HEAD
    vm = pl.BlockSpec(memory_space=pltpu.VMEM)
    return pl.pallas_call(
        functools.partial(attn_forward_kernel, blk),
        grid=(nb,),
        in_specs=[pl.BlockSpec(memory_space=pltpu.SMEM), vm, vm, vm, vm],
        out_specs=[vm, vm, vm],
        out_shape=[jax.ShapeDtypeStruct((3, rows, width), bf16),
                   jax.ShapeDtypeStruct((rows, width), bf16),
                   jax.ShapeDtypeStruct((nb, 8, blk), f32)],
        scratch_shapes=[pltpu.VMEM((heads, blk, 128), f32), pltpu.VMEM((heads, blk, 128), f32)],
        compiler_params=pltpu.CompilerParams(vmem_limit_bytes=56 << 20),
        cost_estimate=pl.CostEstimate(flops=12_000_000_000, transcendentals=0, bytes_accessed=12_000_000),
        name="attn_forward",
    )(info, own, oth, w, b)


def attn_backward_kernel(blk, info, qkv_ref, att_ref, gown_ref, goth_ref, lse_ref, out_ref, g_ref, delta_ref, dq_ref, dk_ref, dv_ref):
    kb = pl.program_id(0)
    nb = pl.num_programs(0)
    half = gown_ref.shape[0]
    width = gown_ref.shape[1]
    heads = width // HEAD
    side, count = info[0], info[1]

    def place(b):
        return pl.multiple_of(lax.rem(b + side * (nb // 2), nb) * blk, blk)

    @pl.when(kb == 0)
    def _():
        g_ref[pl.ds(0, half), :] = gown_ref[...]
        g_ref[pl.ds(half, half), :] = goth_ref[...]
        dq_ref[...] = jnp.zeros_like(dq_ref)
        pick = (lax.broadcasted_iota(jnp.int32, (8, width), 1) // HEAD
                == lax.broadcasted_iota(jnp.int32, (8, width), 0)).astype(bf16)

        def deltas(b, _):
            at = place(b)
            prod = g_ref[pl.ds(at, blk), :].astype(f32) * att_ref[pl.ds(at, blk), :].astype(f32)
            high = prod.astype(bf16)
            low = (prod - high.astype(f32)).astype(bf16)
            delta_ref[b] = (lax.dot_general(pick, high, NT, preferred_element_type=f32)
                            + lax.dot_general(pick, low, NT, preferred_element_type=f32))
            return 0
        lax.fori_loop(0, nb, deltas, 0)

    lane_lo = lax.broadcasted_iota(jnp.int32, (blk, 128), 1) < HEAD
    k_at = place(kb)

    def block(qb, masked):
        q_at = place(qb)
        if masked:
            ki = lax.broadcasted_iota(jnp.int32, (blk, blk), 0)
            qi = lax.broadcasted_iota(jnp.int32, (blk, blk), 1)
            keep = ki <= qi
        for p in range(width // 128):
            cols = pl.ds(128 * p, 128)
            q = qkv_ref[0, pl.ds(q_at, blk), cols]
            g = g_ref[pl.ds(q_at, blk), cols]
            k = qkv_ref[1, pl.ds(k_at, blk), cols]
            v = qkv_ref[2, pl.ds(k_at, blk), cols]
            dk = dv = dq = None
            for h in range(2):
                mine = lane_lo if h == 0 else ~lane_lo
                head = 2 * p + h
                kh = jnp.where(mine, k, bf16(0))
                vh = jnp.where(mine, v, bf16(0))
                s = lax.dot_general(kh, q, NT, preferred_element_type=f32) * LOG2E
                e = jnp.exp2(s - lse_ref[qb, pl.ds(head, 1), :])
                if masked:
                    e = jnp.where(keep, e, 0.0)
                dp = lax.dot_general(vh, g, NT, preferred_element_type=f32)
                ds = (e * (dp - delta_ref[qb, pl.ds(head, 1), :])).astype(bf16)
                e = e.astype(bf16)
                dv1 = jnp.dot(e, jnp.where(mine, g, bf16(0)), preferred_element_type=f32)
                dk1 = jnp.dot(ds, jnp.where(mine, q, bf16(0)), preferred_element_type=f32)
                dq1 = lax.dot_general(ds, kh, TN, preferred_element_type=f32)
                dk, dv, dq = (dk1, dv1, dq1) if h == 0 else (dk + dk1, dv + dv1, dq + dq1)
            if masked:
                dk_ref[:, cols] = dk
                dv_ref[:, cols] = dv
            else:
                dk_ref[:, cols] += dk
                dv_ref[:, cols] += dv
            dq_ref[pl.ds(q_at, blk), cols] += dq

    block(kb, True)
    last = ((kb * count // nb) + 1) * nb // count

    def loop(qb, _):
        block(qb, False)
        return 0
    lax.fori_loop(kb + 1, last, loop, 0)
    out_ref[1, pl.ds(k_at, blk), :] = dk_ref[...].astype(bf16)
    out_ref[2, pl.ds(k_at, blk), :] = dv_ref[...].astype(bf16)

    out_ref[0, pl.ds(k_at, blk), :] = (dq_ref[pl.ds(k_at, blk), :] * 0.125).astype(bf16)


def attn_backward(info, qkv, att, gown, goth, lse, blk=512):
    rows, width = att.shape
    nb = rows // blk
    vm = pl.BlockSpec(memory_space=pltpu.VMEM)
    return pl.pallas_call(
        functools.partial(attn_backward_kernel, blk),
        grid=(nb,),
        in_specs=[pl.BlockSpec(memory_space=pltpu.SMEM)] + [vm] * 5,
        out_specs=vm,
        out_shape=jax.ShapeDtypeStruct((3, rows, width), bf16),
        scratch_shapes=[pltpu.VMEM((rows, width), bf16), pltpu.VMEM((nb, 8, blk), f32),
                        pltpu.VMEM((rows, width), f32), pltpu.VMEM((blk, width), f32),
                        pltpu.VMEM((blk, width), f32)],
        compiler_params=pltpu.CompilerParams(vmem_limit_bytes=56 << 20),
        cost_estimate=pl.CostEstimate(flops=30_000_000_000, transcendentals=0, bytes_accessed=14_000_000),
        name="attn_backward",
    )(info, qkv, att, gown, goth, lse)


DEPTH = 12
EPSILON = 1e-05
BRANCH = 1.0 / math.sqrt(DEPTH)
GELU_C = math.sqrt(2.0 / math.pi)
SWAP = ((0, 1), (1, 0))


def to_peer(v):
    return lax.ppermute(v, "tensor", SWAP)


def row_stats(v):
    centre = jnp.mean(v, axis=-1, keepdims=True)
    centred = v - centre
    inv = lax.rsqrt(jnp.mean(centred * centred, axis=-1, keepdims=True) + EPSILON)
    return centre, inv


def norm_back(e, gain, h, inv):
    eg = e * gain
    return inv * (eg - jnp.mean(eg, axis=-1, keepdims=True)
                  - h * jnp.mean(eg * h, axis=-1, keepdims=True))


def add16(a, b):
    return (a.astype(f32) + b.astype(f32)).astype(bf16)


def dot32(a, b):
    return jnp.dot(a, b, preferred_element_type=f32)


def dot_nt(a, b):
    return lax.dot_general(a, b, NT, preferred_element_type=f32)


def dot_tn(a, b):
    return lax.dot_general(a, b, TN, preferred_element_type=f32)


def xor_step(v, size, bit):
    return lax.ppermute(v, "dp", [(i, i ^ (1 << bit)) for i in range(size)])


def sum_small(v, size):
    for bit in range(size.bit_length() - 1):
        v = v + xor_step(v, size, bit)
    return v


def halving_sum(v, size, me):
    bits = size.bit_length() - 1
    for bit in range(bits):
        half = v.shape[0] // 2
        side = (me >> bit) & 1
        keep = lax.dynamic_slice_in_dim(v, side * half, half, 0)
        send = lax.dynamic_slice_in_dim(v, (1 - side) * half, half, 0)
        v = add16(keep, xor_step(send, size, bit))
    for bit in reversed(range(bits)):
        side = (me >> bit) & 1
        other = xor_step(v, size, bit)
        v = jnp.where(side == 0, jnp.concatenate([v, other]), jnp.concatenate([other, v]))
    return v


def ring_plan(size):
    chips = size // 2
    order = list(range(0, chips, 2)) + list(range(1, chips, 2))[::-1]
    table = [0] * size
    pairs = []
    for p, chip in enumerate(order):
        table[2 * chip] = p
        table[2 * chip + 1] = (chips - p) % chips
        pairs.append((2 * chip, 2 * order[(p + 1) % chips]))
        pairs.append((2 * chip + 1, 2 * order[(p - 1) % chips] + 1))
    return chips, table, pairs


def ring_reduce(first, second, size, me):
    chips, table, pairs = ring_plan(size)
    core = me % 2
    send = jnp.where(core == 0, second, first)
    keep = jnp.where(core == 0, first, second)
    mate = xor_step(send, size, 0)
    rows, width = first.shape[1:]
    ch = rows // chips
    keep = add16(keep, mate).reshape(2, chips, ch, width)
    pos = jnp.array(table, jnp.int32)[me]

    def chunk(i):
        return lax.dynamic_index_in_dim(keep, lax.rem(i + 2 * chips, chips), 1, keepdims=False)

    moving = chunk(pos)
    for s in range(chips - 1):
        moving = add16(lax.ppermute(moving, "dp", pairs), chunk(pos - s - 1))
    done = add16(moving[0], to_peer(moving[1]))
    full = jnp.zeros((chips, ch, width), bf16)
    full = lax.dynamic_update_index_in_dim(full, done, lax.rem(pos + 1, chips), 0)
    for s in range(chips - 1):
        done = lax.ppermute(done, "dp", pairs)
        full = lax.dynamic_update_index_in_dim(full, done, lax.rem(pos - s + chips, chips), 0)
    full = full.reshape(rows, width)
    other = xor_step(full, size, 0)
    return jnp.where(core == 0, full, other), jnp.where(core == 0, other, full)


def gelu_pair(v):
    t = jnp.tanh(GELU_C * (v + 0.044715 * v * v * v))
    return 0.5 * v * (1.0 + t), 0.5 * (1.0 + t) + 0.5 * v * (1.0 - t * t) * (
        GELU_C * (1.0 + 3.0 * 0.044715 * v * v))


def local(
    tokens,
    seq_count,
    first_gain,
    first_shift,
    heads_weight,
    heads_bias,
    mixing_weight,
    mixing_bias,
    second_gain,
    second_shift,
    up_weight,
    up_bias,
    down_weight,
    down_bias,
    cotangent,
):
    size = lax.axis_size("dp")
    me = lax.axis_index("dp")
    side = lax.axis_index("tensor")
    info = jnp.stack([side.astype(jnp.int32), seq_count[0]])
    half, dim = tokens.shape
    width = heads_weight.shape[2]
    hidden = up_weight.shape[1]

    pu, pd, pm = dim // size, hidden // size, width // size
    piece = jnp.concatenate([
        lax.dynamic_slice(up_weight, (me * pu, 0), (pu, hidden // 2)),
        lax.dynamic_slice(up_weight, (me * pu, hidden // 2), (pu, hidden // 2)),
        lax.dynamic_slice_in_dim(down_weight, me * pd, pd, 0),
        lax.dynamic_slice_in_dim(mixing_weight, me * pm, pm, 0)])
    packed = lax.all_gather(to_peer(piece), "dp", axis=0)
    up_other = jnp.concatenate([packed[:, :pu].reshape(dim, hidden // 2),
                                packed[:, pu:2 * pu].reshape(dim, hidden // 2)], axis=1)
    down_other = packed[:, 2 * pu:2 * pu + pd].reshape(hidden, dim)
    mix_other = packed[:, 2 * pu + pd:].reshape(width, dim)
    up_bias_other = to_peer(up_bias)

    x = tokens.astype(f32)
    centre1, inv1 = row_stats(x)
    a1 = ((x - centre1) * inv1 * first_gain + first_shift).astype(bf16)
    a1_other = to_peer(a1)
    bias3 = jnp.stack([heads_bias[0], jnp.zeros_like(heads_bias[0]), heads_bias[1]])
    qkv, att, lse = attn_forward(info, a1, a1_other, heads_weight, bias3)
    att_mine = att[:half]
    att_recv = to_peer(att[half:])
    middle = x + BRANCH * (dot32(att_mine, mixing_weight) + dot32(att_recv, mix_other) + mixing_bias)
    centre2, inv2 = row_stats(middle)
    h2 = (middle - centre2) * inv2
    a2 = (h2 * second_gain + second_shift).astype(bf16)

    g_out = cotangent.astype(f32)
    grad_mlp = (BRANCH * g_out).astype(bf16)
    down_sum = 0.0
    grad_a2 = 0.0
    grads_up, grads_down, bias_up = [], [], []
    for up, bias, down in ((up_weight, up_bias, down_weight), (up_other, up_bias_other, down_other)):
        pre = dot32(a2, up) + bias
        act, slope = gelu_pair(pre)
        act = act.astype(bf16)
        down_sum += dot32(act, down)
        grad_pre = (dot_nt(grad_mlp, down) * slope).astype(bf16)
        grads_down.append(dot_tn(act, grad_mlp).astype(bf16))
        grads_up.append(jnp.concatenate([dot_tn(a2, grad_pre[:, :hidden // 2]),
                                         dot_tn(a2, grad_pre[:, hidden // 2:])]).astype(bf16))
        bias_up.append(jnp.sum(grad_pre, axis=0, dtype=f32).reshape(2, dim))
        grad_a2 += dot_nt(grad_pre, up)
    result = (middle + BRANCH * (down_sum + down_bias)).astype(bf16)
    grad_down, grad_up = ring_reduce(jnp.stack(grads_down), jnp.stack(grads_up), size, me)

    grad_middle = g_out + norm_back(grad_a2, second_gain, h2, inv2)
    grad_attn = (BRANCH * grad_middle).astype(bf16)
    g_own = dot_nt(grad_attn, mixing_weight).astype(bf16)
    g_other = to_peer(dot_nt(grad_attn, mix_other).astype(bf16))
    small = jnp.concatenate([
        jnp.stack([BRANCH * jnp.sum(g_out, axis=0), jnp.sum(grad_a2 * h2, axis=0),
                   jnp.sum(grad_a2, axis=0), BRANCH * jnp.sum(grad_middle, axis=0)])] + bias_up)
    small = sum_small(small, size)
    small = small[:6] + to_peer(jnp.concatenate([small[:4], small[6:8]]))
    grad_mix = add16(dot_tn(att_mine, grad_attn), to_peer(dot_tn(att_recv, grad_attn).astype(bf16)))

    gqkv = attn_backward(info, qkv, att, g_own, g_other, lse)
    gq_mine, gq_other = gqkv[:, :half], gqkv[:, half:]

    def back_heads(gq):
        return sum(dot_nt(gq[j], heads_weight[j]) for j in range(3))

    sent = to_peer(back_heads(gq_other).astype(bf16))
    grad_a1 = back_heads(gq_mine) + sent.astype(f32)
    grad_heads = [(dot_tn(a1, gq_mine[j]) + dot_tn(a1_other, gq_other[j])).astype(bf16) for j in range(3)]
    tail = jnp.concatenate(grad_heads + [grad_mix[:, :width], grad_mix[:, width:]])
    tail = halving_sum(tail, size, me)

    h1 = (x - centre1) * inv1
    grad_tokens = (grad_middle + norm_back(grad_a1, first_gain, h1, inv1)).astype(bf16)
    grad_hb = jnp.concatenate([jnp.sum(gqkv[0], axis=0, dtype=f32), jnp.sum(gqkv[2], axis=0, dtype=f32)])
    last = jnp.stack([jnp.sum(grad_a1 * h1, axis=0), jnp.sum(grad_a1, axis=0), grad_hb])
    last = sum_small(last, size)
    first_two = last[:2] + to_peer(last[:2])
    groups = 1.0 / size
    first_two = first_two * groups
    small = small * groups
    tail = tail.astype(f32) * groups
    grad_up = grad_up.astype(f32) * groups
    return (
        result,
        grad_tokens,
        first_two[0],
        first_two[1],
        tail[:3 * dim].reshape(3, dim, width),
        last[2].reshape(2, width) * groups,
        jnp.concatenate([tail[3 * dim:3 * dim + width], tail[3 * dim + width:]], axis=1),
        small[3],
        small[1],
        small[2],
        jnp.concatenate([grad_up[:dim], grad_up[dim:]], axis=1),
        small[4:6].reshape(hidden),
        grad_down.astype(f32) * groups,
        small[0],
    )


def solution(mesh):
    placed = (
        P(("dp", "tensor"), None),
        P("dp"),
        P(),
        P(),
        P(None, None, "tensor"),
        P(None, "tensor"),
        P("tensor", None),
        P(),
        P(),
        P(),
        P(None, "tensor"),
        P("tensor"),
        P("tensor", None),
        P(),
        P(("dp", "tensor"), None),
    )
    return jax.shard_map(
        local,
        mesh=mesh,
        in_specs=placed,
        out_specs=(
            P(("dp", "tensor"), None),
            P(("dp", "tensor"), None),
            P(),
            P(),
            P(None, None, "tensor"),
            P(None, "tensor"),
            P("tensor", None),
            P(),
            P(),
            P(),
            P(None, "tensor"),
            P("tensor"),
            P("tensor", None),
            P(),
        ),
        check_vma=False,
    )
```

time: 996 us -> 478 us (0.48)
  waiting for transfers between devices: 438 us -> 158 us
  matrix products: 261 us -> 86 us
  blocking collectives: 102 us -> 0 us
  Pallas kernels: 0 us -> 99.4 us
  other arithmetic: 134 us -> 37.5 us
  starting transfers between devices: 0.37 us -> 32.2 us
  between operations: 16.1 us -> 27 us
    dot_general x36 -> x32, matrix products: 261 us -> 86 us  [the longest x14 37.9 us: dot_tn(): return lax.dot_general(a, b, TN, preferred_element_type=f32)]
    all_gather x4 -> x1, waiting for transfers between devices: 161 us -> 0.02 us  [local(): packed = lax.all_gather(to_peer(piece), 'dp', axis=0)]
    psum x1 -> x0, waiting for transfers between devices: 159 us -> none  [local(): lax.psum((grad_heads, grad_heads_bias, grad_mixing, grad_up, grad_up_bias...]
    ppermute x0 -> x42, waiting for transfers between devices: none -> 158 us  [the longest x10 55 us: to_peer(): return lax.ppermute(v, 'tensor', SWAP)]
    reduce_scatter x4 -> x0, waiting for transfers between devices: 118 us -> none  [the longest x1 43.5 us: local(): lax.psum_scatter(jnp.dot(attended, mixing_weight, preferred_element_type=...]
    psum x2 -> x0, blocking collectives: 102 us -> none  [the longest x1 63.6 us: local(): lax.psum((grad_heads, grad_heads_bias, grad_mixing, grad_up, grad_up_bias...]
    pallas_call x0 -> x2, Pallas kernels: none -> 99.4 us  [the longest x1 53.3 us: attn_backward(): pl.pallas_call(functools.partial(attn_backward_kernel, blk), grid=(nb,),...]
    convert_element_type x8 -> x16, other arithmetic: 57.5 us -> 10.5 us  [the longest x12 5.71 us: add16(): return (a.astype(f32) + b.astype(f32)).astype(bf16)]
  transfers between devices with their start and end apart: 9 -> 43, of which waited for: 8 -> 25; matrix products, arithmetic and copies ran while one was open for 8% -> 24% of each run, Pallas kernels for 0% -> 21%
where the time goes in v1:
time: 478 us; the launch traced here: 470 us
  waiting for transfers between devices  158 us (33%)
  Pallas kernels  99.4 us (21%)
  matrix products  86 us (18%)
  other arithmetic  37.5 us (8%)
  starting transfers between devices  32.2 us (7%)
  local copies, waits for them, and re-layouts  30.1 us (6%)
  between operations  27 us (6%)
    ppermute x10, waiting for transfers between devices, to_peer(): return lax.ppermute(v, 'tensor', SWAP)  55 us
    pallas_call x1, Pallas kernels, attn_backward(): pl.pallas_call(functools.partial(attn_backward_kernel, blk), grid=(nb,),...  53.3 us
    ppermute x7, waiting for transfers between devices, ring_reduce(): moving = add16(lax.ppermute(moving, 'dp', pairs), chunk(pos - s - 1))  49.5 us
    pallas_call x1, Pallas kernels, attn_forward(): pl.pallas_call(functools.partial(attn_forward_kernel, blk), grid=(nb,), i...  46.1 us
    ppermute x7, waiting for transfers between devices, ring_reduce(): done = lax.ppermute(done, 'dp', pairs)  38.5 us
    dot_general x14, matrix products, dot_tn(): return lax.dot_general(a, b, TN, preferred_element_type=f32)  37.9 us
    dot_general x12, matrix products, dot_nt(): return lax.dot_general(a, b, NT, preferred_element_type=f32)  29.2 us
    dot_general x6, matrix products, dot32(): return jnp.dot(a, b, preferred_element_type=f32)  18.9 us
  transfers between devices with their start and end apart: 43, of which 25 were waited for; matrix products, arithmetic and copies ran while one was open for 24% of the time, Pallas kernels for 21%

profile of v1, /device:TPU:0, one launch (start us, length us, event | category | flops | bytes accessed | tf_op | source)
XLA Modules:
  0.0 470.4 jit_solution(7252423443511834437)
XLA Ops:
  12.9 7.8 %collective-permute-done.2 = bf16[216,768]{1,0:T(8,128)(2,1)S(1)} collective-permute-done((bf16[216,768]{1,0:T(8,128)(2,1)S(1)}, bf16[216,768]{1,0:T(8,128)(2,1)S(1)}, u32[]{:S(2)}, u32[]{:S(2)}) %collective-permute-start.2) | collective-permute-done | bytes 331808 | tf_op jit(solution)/shard_map/ppermute | solution.py:228
  30.9 32.1 %collective-permute-done.oth_ref = bf16[1024,768]{1,0:T(8,128)(2,1)} collective-permute-done((bf16[1024,768]{1,0:T(8,128)(2,1)}, bf16[1024,768]{1,0:T(8,128)(2,1)}, u32[]{:S(2)}, u32[]{:S(2)}) %collective-permute-start) | collective-permute-done | bytes 1572896 | tf_op jit(solution)/shard_map/ppermute | solution.py:228
  63.0 46.1 %attn_forward.1 = (bf16[3,2048,384]{2,1,0:T(8,128)(2,1)}, bf16[2048,384]{1,0:T(8,128)(2,1)}, f32[4,8,512]{2,1,0:T(8,128)}) custom-call(s32[2]{0:T(128)} %pad_add_fusion.info, bf16[1024,768]{1,0:T(8,128)(2,1)} %fusion.23.own_ref, bf16[1024,768]{1,0:T(8,128)(2,1)} %collective-permute-done.oth_ref, bf16[3,768,384]{2,1,0:T(8,128)(2,1)} %w_ref.1, ...), custom_call_target="tpu_custom_call" | custom-call | flops 12000000000 | bytes 12000000 | tf_op jit(solution)/shard_map/attn_forward/pallas_call | solution.py:104
  145.6 6.2 %convert_reduce_fusion.1 = (f32[1536]{0:T(1024)S(1)}, bf16[1024,1536]{1,0:T(8,128)(2,1)S(1)}) fusion(f32[1024,1536]{1,0:T(8,128)S(1)} %get-tuple-element.57, f32[1536]{0:T(1024)S(1)} %copy-done.46, bf16[1536,768]{1,0:T(8,128)(2,1)S(1)} %copy-done, bf16[1024,768]{1,0:T(8,128)(2,1)S(1)} %copy-done.28), kind=kOutput, calls=%fused_computation.22 | convolution fusion | flops 2452879872 | bytes 13381632 | tf_op jit(solution)/shard_map/dot_general | solution.py:253
  161.1 6.8 %convert_reduce_fusion = (f32[1536]{0:T(1024)S(1)}, bf16[1024,1536]{1,0:T(8,128)(2,1)S(1)}) fusion(f32[1024,1536]{1,0:T(8,128)S(1)} %fusion.54, f32[1536]{0:T(1024)} %collective-permute-done.3, bf16[1536,768]{1,0:T(8,128)(2,1)S(1)} %bitcast.186, bf16[1024,768]{1,0:T(8,128)(2,1)S(1)} %copy-done.28), kind=kOutput, calls=%fused_computation.21 | convolution fusion | flops 2452879872 | bytes 13381632 | tf_op jit(solution)/shard_map/dot_general | solution.py:253
  182.4 7.5 %fusion.33 = bf16[1,1536,768]{2,1,0:T(8,128)(2,1)S(1)} fusion(bf16[1024,768]{1,0:T(8,128)(2,1)} %param.30, f32[1024,1536]{1,0:T(8,128)} %copy-done.49, f32[1536]{0:T(1024)} %collective-permute-done.3), kind=kOutput, calls=%fused_computation.67 | convolution fusion | flops 2435186688 | bytes 10229760 | tf_op jit(solution)/shard_map/dot_general | solution.py:257
  203.7 6.1 %add_convert_fusion.2 = bf16[1024,768]{1,0:T(8,128)(2,1)} fusion(f32[1024,768]{1,0:T(8,128)S(1)} %copy-done.6, f32[1024,768]{1,0:T(8,128)S(1)} %copy-done.54, bf16[1536,768]{1,0:T(8,128)(2,1)S(1)} %bitcast.187, f32[768]{0:T(1024)S(1)} %copy-done.47, f32[1024,1536]{1,0:T(8,128)S(1)} %bitcast.193, f32[1536]{0:T(1024)} %collective-permute-done.3), kind=kOutput, calls=%fused_computation.63 | convolution fusion | flops 2435579904 | bytes 16524288 | tf_op jit(solution)/shard_map/dot_general | solution.py:249
  219.2 53.3 %attn_backward.1 = bf16[3,2048,384]{2,1,0:T(8,128)(2,1)} custom-call(s32[2]{0:T(128)} %pad_add_fusion.info, bf16[3,2048,384]{2,1,0:T(8,128)(2,1)} %get-tuple-element.18.qkv_ref, bf16[2048,384]{1,0:T(8,128)(2,1)} %get-tuple-element.17.att_ref, bf16[1024,384]{1,0:T(8,128)(2,1)} %convolution_convert_fusion.3.gown_ref, ...), custom_call_target="tpu_custom_call" | custom-call | flops 30000001024 | bytes 14000000 | tf_op jit(solution)/shard_map/attn_backward/pallas_call | solution.py:205
  289.9 5.0 %collective-permute-done.26 = bf16[2,192,768]{2,1,0:T(8,128)(2,1)S(1)} collective-permute-done((bf16[2,192,768]{2,1,0:T(8,128)(2,1)S(1)}, bf16[2,192,768]{2,1,0:T(8,128)(2,1)S(1)}, u32[]{:S(2)}, u32[]{:S(2)}) %collective-permute-start.26) | collective-permute-done | bytes 589856 | tf_op jit(solution)/shard_map/ppermute | solution.py:314
  297.7 7.2 %collective-permute-done.27 = bf16[2,192,768]{2,1,0:T(8,128)(2,1)S(1)} collective-permute-done((bf16[2,192,768]{2,1,0:T(8,128)(2,1)S(1)}, bf16[2,192,768]{2,1,0:T(8,128)(2,1)S(1)}, u32[]{:S(2)}, u32[]{:S(2)}) %collective-permute-start.27) | collective-permute-done | bytes 589856 | tf_op jit(solution)/shard_map/ppermute | solution.py:314
  306.4 8.6 %collective-permute-done.28 = bf16[2,192,768]{2,1,0:T(8,128)(2,1)S(1)} collective-permute-done((bf16[2,192,768]{2,1,0:T(8,128)(2,1)S(1)}, bf16[2,192,768]{2,1,0:T(8,128)(2,1)S(1)}, u32[]{:S(2)}, u32[]{:S(2)}) %collective-permute-start.28) | collective-permute-done | bytes 589856 | tf_op jit(solution)/shard_map/ppermute | solution.py:314
  317.3 7.9 %collective-permute-done.29 = bf16[2,192,768]{2,1,0:T(8,128)(2,1)S(1)} collective-permute-done((bf16[2,192,768]{2,1,0:T(8,128)(2,1)S(1)}, bf16[2,192,768]{2,1,0:T(8,128)(2,1)S(1)}, u32[]{:S(2)}, u32[]{:S(2)}) %collective-permute-start.29) | collective-permute-done | bytes 589856 | tf_op jit(solution)/shard_map/ppermute | solution.py:314
  327.4 8.2 %collective-permute-done.30 = bf16[2,192,768]{2,1,0:T(8,128)(2,1)S(1)} collective-permute-done((bf16[2,192,768]{2,1,0:T(8,128)(2,1)S(1)}, bf16[2,192,768]{2,1,0:T(8,128)(2,1)S(1)}, u32[]{:S(2)}, u32[]{:S(2)}) %collective-permute-start.30) | collective-permute-done | bytes 589856 | tf_op jit(solution)/shard_map/ppermute | solution.py:314
  341.2 6.6 %collective-permute-done.31 = bf16[2,192,768]{2,1,0:T(8,128)(2,1)S(1)} collective-permute-done((bf16[2,192,768]{2,1,0:T(8,128)(2,1)S(1)}, bf16[2,192,768]{2,1,0:T(8,128)(2,1)S(1)}, u32[]{:S(2)}, u32[]{:S(2)}) %collective-permute-start.31) | collective-permute-done | bytes 589856 | tf_op jit(solution)/shard_map/ppermute | solution.py:314
  348.6 5.6 %collective-permute-done.13 = bf16[768,384]{1,0:T(8,128)(2,1)S(1)} collective-permute-done((bf16[768,384]{1,0:T(8,128)(2,1)S(1)}, bf16[768,384]{1,0:T(8,128)(2,1)S(1)}, u32[]{:S(2)}, u32[]{:S(2)}) %collective-permute-start.13) | collective-permute-done | bytes 589856 | tf_op jit(solution)/shard_map/ppermute | solution.py:261
  354.5 6.0 %collective-permute-done.32 = bf16[2,192,768]{2,1,0:T(8,128)(2,1)S(1)} collective-permute-done((bf16[2,192,768]{2,1,0:T(8,128)(2,1)S(1)}, bf16[2,192,768]{2,1,0:T(8,128)(2,1)S(1)}, u32[]{:S(2)}, u32[]{:S(2)}) %collective-permute-start.32) | collective-permute-done | bytes 589856 | tf_op jit(solution)/shard_map/ppermute | solution.py:314
  363.6 12.7 %collective-permute-done.33 = bf16[192,768]{1,0:T(8,128)(2,1)S(1)} collective-permute-done((bf16[192,768]{1,0:T(8,128)(2,1)S(1)}, bf16[192,768]{1,0:T(8,128)(2,1)S(1)}, u32[]{:S(2)}, u32[]{:S(2)}) %collective-permute-start.33) | collective-permute-done | bytes 294944 | tf_op jit(solution)/shard_map/ppermute | solution.py:228
  381.0 4.4 collective-permute-done.34
  394.5 4.6 collective-permute-done.36
  404.6 4.4 collective-permute-done.37
  410.5 10.6 %collective-permute-done.38 = bf16[192,768]{1,0:T(8,128)(2,1)S(1)} collective-permute-done((bf16[192,768]{1,0:T(8,128)(2,1)S(1)}, bf16[192,768]{1,0:T(8,128)(2,1)S(1)}, u32[]{:S(2)}, u32[]{:S(2)}) %collective-permute-start.38) | collective-permute-done | bytes 294944 | tf_op jit(solution)/shard_map/ppermute | solution.py:319
  422.5 5.3 %collective-permute-done.39 = bf16[192,768]{1,0:T(8,128)(2,1)S(1)} collective-permute-done((bf16[192,768]{1,0:T(8,128)(2,1)S(1)}, bf16[192,768]{1,0:T(8,128)(2,1)S(1)}, u32[]{:S(2)}, u32[]{:S(2)}) %collective-permute-start.39) | collective-permute-done | bytes 294944 | tf_op jit(solution)/shard_map/ppermute | solution.py:319
  429.2 5.3 %collective-permute-done.40 = bf16[192,768]{1,0:T(8,128)(2,1)S(1)} collective-permute-done((bf16[192,768]{1,0:T(8,128)(2,1)S(1)}, bf16[192,768]{1,0:T(8,128)(2,1)S(1)}, u32[]{:S(2)}, u32[]{:S(2)}) %collective-permute-start.40) | collective-permute-done | bytes 294944 | tf_op jit(solution)/shard_map/ppermute | solution.py:319
  454.4 5.5 %convert_multiply_fusion.1 = (f32[1536,768]{1,0:T(8,128)}, f32[1536,768]{1,0:T(8,128)S(1)}) fusion(bf16[1536,768]{1,0:T(8,128)(2,1)} %collective-permute-done.41, pred[]{:T(512)S(6)} %eq.24, bf16[8,192,768]{2,1,0:T(8,128)(2,1)} %bitcast_dynamic-update-slice_fusion), kind=kLoop, calls=%fused_computation.34 | loop fusion | flops 7077888 | bytes 14155777 | tf_op jit(solution)/shard_map/mul | solution.py:449
  (316 shorter events, 169.6 us)
Async XLA Ops:
  7.2 117.2 %all-gather.3.cloned.1.call-start = ((), (), s32[]{:S(2)}) async-start(), calls=%async_computation | async-start | bytes 5640192 | tf_op jit(solution)/shard_map/all_gather | solution.py:363
  9.9 10.9 %collective-permute-start.2 = (bf16[216,768]{1,0:T(8,128)(2,1)S(1)}, bf16[216,768]{1,0:T(8,128)(2,1)S(1)}, u32[]{:S(2)}, u32[]{:S(2)}) collective-permute-start(bf16[216,768]{1,0:T(8,128)(2,1)S(1)} %pad_maximum_fusion.6), channel_id=1, source_target_pairs={{0,1},{1,0},{2,3},{3,2},{4,5},{5,4},{6,7},{7,6},{8,9},{9,8},{10,11... | collective-permute-start | bytes 995336 | tf_op jit(solution)/shard_map/ppermute | solution.py:228
  27.2 35.9 %collective-permute-start = (bf16[1024,768]{1,0:T(8,128)(2,1)}, bf16[1024,768]{1,0:T(8,128)(2,1)}, u32[]{:S(2)}, u32[]{:S(2)}) collective-permute-start(bf16[1024,768]{1,0:T(8,128)(2,1)} %fusion.23.own_ref), channel_id=1, source_target_pairs={{0,1},{1,0},{2,3},{3,2},{4,5},{5,4},{6,7},{7,6},{8,9},{9,8},{10,11... | collective-permute-start | bytes 4718600 | tf_op jit(solution)/shard_map/ppermute | solution.py:228
  111.2 16.1 %collective-permute-start.1 = (bf16[1024,384]{1,0:T(8,128)(2,1)}, bf16[1024,384]{1,0:T(8,128)(2,1)S(1)}, u32[]{:S(2)}, u32[]{:S(2)}) collective-permute-start(bf16[1024,384]{1,0:T(8,128)(2,1)} %slice.153), channel_id=1, source_target_pairs={{0,1},{1,0},{2,3},{3,2},{4,5},{5,4},{6,7},{7,6},{8,9},{9,8},{10,11... | collective-permute-start | bytes 2359304 | tf_op jit(solution)/shard_map/ppermute | solution.py:228
  112.7 48.4 %collective-permute-start.3 = (f32[1536]{0:T(1024)S(1)}, f32[1536]{0:T(1024)}, u32[]{:S(2)}, u32[]{:S(2)}) collective-permute-start(f32[1536]{0:T(1024)S(1)} %copy-done.46), channel_id=1, source_target_pairs={{0,1},{1,0},{2,3},{3,2},{4,5},{5,4},{6,7},{7,6},{8,9},{9,8},{10,11... | collective-permute-start | bytes 18440 | tf_op jit(solution)/shard_map/ppermute | solution.py:228
  178.5 40.7 %collective-permute-start.4 = (bf16[1024,384]{1,0:T(8,128)(2,1)}, bf16[1024,384]{1,0:T(8,128)(2,1)}, u32[]{:S(2)}, u32[]{:S(2)}) collective-permute-start(bf16[1024,384]{1,0:T(8,128)(2,1)} %convolution_convert_fusion.2), channel_id=1, source_target_pairs={{0,1},{1,0},{2,3},{3,2},{4,5},{5,4},{6,7},{7,6},{8,9},{9,8},{10,11... | collective-permute-start | bytes 2359304 | tf_op jit(solution)/shard_map/ppermute | solution.py:228
  181.6 35.0 %collective-permute-start.11 = (bf16[384,768]{1,0:T(8,128)(2,1)}, bf16[384,768]{1,0:T(8,128)(2,1)}, u32[]{:S(2)}, u32[]{:S(2)}) collective-permute-start(bf16[384,768]{1,0:T(8,128)(2,1)} %convolution_convert_fusion.4), channel_id=1, source_target_pairs={{0,1},{1,0},{2,3},{3,2},{4,5},{5,4},{6,7},{7,6},{8,9},{9,8},{10,11... | collective-permute-start | bytes 1769480 | tf_op jit(solution)/shard_map/ppermute | solution.py:228
  200.5 80.2 %collective-permute-start.25 = (bf16[2,1536,768]{2,1,0:T(8,128)(2,1)}, bf16[2,1536,768]{2,1,0:T(8,128)(2,1)}, u32[]{:S(2)}, u32[]{:S(2)}) collective-permute-start(bf16[2,1536,768]{2,1,0:T(8,128)(2,1)} %broadcast_select_fusion), channel_id=1, source_target_pairs={{0,2},{2,0},{4,6},{6,4},{8,10},{10,8},{12,14},{14,12},{16,18},{18,... | collective-permute-start | bytes 14155784 | tf_op jit(solution)/shard_map/ppermute | solution.py:261
  305.3 30.7 %collective-permute-start.12 = (bf16[1536,384]{1,0:T(8,128)(2,1)S(1)}, bf16[1536,384]{1,0:T(8,128)(2,1)S(1)}, u32[]{:S(2)}, u32[]{:S(2)}) collective-permute-start(bf16[1536,384]{1,0:T(8,128)(2,1)S(1)} %constant_dynamic-slice_fusion.3), channel_id=1, source_target_pairs={{0,2},{2,0},{4,6},{6,4},{8,10},{10,8},{12,14},{14,12},{16,18},{18,... | collective-permute-start | bytes 3538952 | tf_op jit(solution)/shard_map/ppermute | solution.py:261
  325.3 10.2 %collective-permute-start.30 = (bf16[2,192,768]{2,1,0:T(8,128)(2,1)S(1)}, bf16[2,192,768]{2,1,0:T(8,128)(2,1)S(1)}, u32[]{:S(2)}, u32[]{:S(2)}) collective-permute-start(bf16[2,192,768]{2,1,0:T(8,128)(2,1)S(1)} %fusion.77), channel_id=1, source_target_pairs={{0,8},{2,6},{8,16},{10,2},{16,24},{18,10},{24,28},{26,18},{28,20},... | collective-permute-start | bytes 1769480 | tf_op jit(solution)/shard_map/ppermute | solution.py:314
  335.7 12.2 %collective-permute-start.31 = (bf16[2,192,768]{2,1,0:T(8,128)(2,1)S(1)}, bf16[2,192,768]{2,1,0:T(8,128)(2,1)S(1)}, u32[]{:S(2)}, u32[]{:S(2)}) collective-permute-start(bf16[2,192,768]{2,1,0:T(8,128)(2,1)S(1)} %fusion.76), channel_id=1, source_target_pairs={{0,8},{2,6},{8,16},{10,2},{16,24},{18,10},{24,28},{26,18},{28,20},... | collective-permute-start | bytes 1769480 | tf_op jit(solution)/shard_map/ppermute | solution.py:314
  336.4 17.8 %collective-permute-start.13 = (bf16[768,384]{1,0:T(8,128)(2,1)S(1)}, bf16[768,384]{1,0:T(8,128)(2,1)S(1)}, u32[]{:S(2)}, u32[]{:S(2)}) collective-permute-start(bf16[768,384]{1,0:T(8,128)(2,1)S(1)} %constant_dynamic-slice_fusion.2), channel_id=1, source_target_pairs={{0,4},{2,6},{4,0},{6,2},{8,12},{10,14},{12,8},{14,10},{16,20},{18,... | collective-permute-start | bytes 1769480 | tf_op jit(solution)/shard_map/ppermute | solution.py:261
  339.5 46.6 %collective-permute-start.5 = (bf16[1024,768]{1,0:T(8,128)(2,1)S(1)}, bf16[1024,768]{1,0:T(8,128)(2,1)S(1)}, u32[]{:S(2)}, u32[]{:S(2)}) collective-permute-start(bf16[1024,768]{1,0:T(8,128)(2,1)S(1)} %add_convert_fusion.1), channel_id=1, source_target_pairs={{0,1},{1,0},{2,3},{3,2},{4,5},{5,4},{6,7},{7,6},{8,9},{9,8},{10,11... | collective-permute-start | bytes 4718600 | tf_op jit(solution)/shard_map/ppermute | solution.py:228
  348.0 12.5 %collective-permute-start.32 = (bf16[2,192,768]{2,1,0:T(8,128)(2,1)S(1)}, bf16[2,192,768]{2,1,0:T(8,128)(2,1)S(1)}, u32[]{:S(2)}, u32[]{:S(2)}) collective-permute-start(bf16[2,192,768]{2,1,0:T(8,128)(2,1)S(1)} %fusion.75), channel_id=1, source_target_pairs={{0,8},{2,6},{8,16},{10,2},{16,24},{18,10},{24,28},{26,18},{28,20},... | collective-permute-start | bytes 1769480 | tf_op jit(solution)/shard_map/ppermute | solution.py:314
  360.7 15.6 %collective-permute-start.33 = (bf16[192,768]{1,0:T(8,128)(2,1)S(1)}, bf16[192,768]{1,0:T(8,128)(2,1)S(1)}, u32[]{:S(2)}, u32[]{:S(2)}) collective-permute-start(bf16[192,768]{1,0:T(8,128)(2,1)S(1)} %slice_bitcast_fusion.20), channel_id=1, source_target_pairs={{0,1},{1,0},{2,3},{3,2},{4,5},{5,4},{6,7},{7,6},{8,9},{9,8},{10,11... | collective-permute-start | bytes 884744 | tf_op jit(solution)/shard_map/ppermute | solution.py:228
  363.5 15.9 %collective-permute-start.15 = (bf16[192,384]{1,0:T(8,128)(2,1)S(1)}, bf16[192,384]{1,0:T(8,128)(2,1)S(1)}, u32[]{:S(2)}, u32[]{:S(2)}) collective-permute-start(bf16[192,384]{1,0:T(8,128)(2,1)S(1)} %constant_dynamic-slice_fusion), channel_id=1, source_target_pairs={{0,16},{2,18},{4,20},{6,22},{8,24},{10,26},{12,28},{14,30},{16,0},... | collective-permute-start | bytes 442376 | tf_op jit(solution)/shard_map/ppermute | solution.py:261
  379.4 13.4 %collective-permute-start.16 = (bf16[192,384]{1,0:T(8,128)(2,1)S(1)}, bf16[192,384]{1,0:T(8,128)(2,1)S(1)}, u32[]{:S(2)}, u32[]{:S(2)}) collective-permute-start(bf16[192,384]{1,0:T(8,128)(2,1)S(1)} %add_convert_fusion.7), channel_id=1, source_target_pairs={{0,16},{2,18},{4,20},{6,22},{8,24},{10,26},{12,28},{14,30},{16,0},... | collective-permute-start | bytes 442376 | tf_op jit(solution)/shard_map/ppermute | solution.py:261
  388.3 11.4 %collective-permute-start.6 = (f32[3,768]{1,0:T(4,128)S(1)}, f32[3,768]{1,0:T(4,128)S(1)}, u32[]{:S(2)}, u32[]{:S(2)}) collective-permute-start(f32[3,768]{1,0:T(4,128)S(1)} %pad_maximum_fusion.8), channel_id=1, source_target_pairs={{0,2},{2,0},{4,6},{6,4},{8,10},{10,8},{12,14},{14,12},{16,18},{18,... | collective-permute-start | bytes 27656 | tf_op jit(solution)/shard_map/ppermute | solution.py:261
  392.9 9.9 %collective-permute-start.17 = (bf16[384,384]{1,0:T(8,128)(2,1)S(1)}, bf16[384,384]{1,0:T(8,128)(2,1)S(1)}, u32[]{:S(2)}, u32[]{:S(2)}) collective-permute-start(bf16[384,384]{1,0:T(8,128)(2,1)S(1)} %maximum_select_fusion.3), channel_id=1, source_target_pairs={{0,8},{2,10},{4,12},{6,14},{8,0},{10,2},{12,4},{14,6},{16,24},{18,... | collective-permute-start | bytes 884744 | tf_op jit(solution)/shard_map/ppermute | solution.py:261
  399.7 36.5 %collective-permute-start.7 = (f32[3,768]{1,0:T(4,128)S(1)}, f32[3,768]{1,0:T(4,128)S(1)}, u32[]{:S(2)}, u32[]{:S(2)}) collective-permute-start(f32[3,768]{1,0:T(4,128)S(1)} %fusion.117), channel_id=1, source_target_pairs={{0,4},{2,6},{4,0},{6,2},{8,12},{10,14},{12,8},{14,10},{16,20},{18,... | collective-permute-start | bytes 27656 | tf_op jit(solution)/shard_map/ppermute | solution.py:261
  403.1 32.2 %collective-permute-start.18 = (bf16[768,384]{1,0:T(8,128)(2,1)S(1)}, bf16[768,384]{1,0:T(8,128)(2,1)S(1)}, u32[]{:S(2)}, u32[]{:S(2)}) collective-permute-start(bf16[768,384]{1,0:T(8,128)(2,1)S(1)} %maximum_select_fusion.2), channel_id=1, source_target_pairs={{0,4},{2,6},{4,0},{6,2},{8,12},{10,14},{12,8},{14,10},{16,20},{18,... | collective-permute-start | bytes 1769480 | tf_op jit(solution)/shard_map/ppermute | solution.py:261
  409.0 12.0 %collective-permute-start.38 = (bf16[192,768]{1,0:T(8,128)(2,1)S(1)}, bf16[192,768]{1,0:T(8,128)(2,1)S(1)}, u32[]{:S(2)}, u32[]{:S(2)}) collective-permute-start(bf16[192,768]{1,0:T(8,128)(2,1)S(1)} %collective-permute-done.37), channel_id=1, source_target_pairs={{0,8},{2,6},{8,16},{10,2},{16,24},{18,10},{24,28},{26,18},{28,20},... | collective-permute-start | bytes 884744 | tf_op jit(solution)/shard_map/ppermute | solution.py:319
  435.2 19.1 %collective-permute-start.41 = (bf16[1536,768]{1,0:T(8,128)(2,1)}, bf16[1536,768]{1,0:T(8,128)(2,1)}, u32[]{:S(2)}, u32[]{:S(2)}) collective-permute-start(bf16[1536,768]{1,0:T(8,128)(2,1)} %bitcast.57), channel_id=1, source_target_pairs={{0,2},{2,0},{4,6},{6,4},{8,10},{10,8},{12,14},{14,12},{16,18},{18,... | collective-permute-start | bytes 7077896 | tf_op jit(solution)/shard_map/ppermute | solution.py:261
  435.6 13.3 %collective-permute-start.19 = (bf16[1536,384]{1,0:T(8,128)(2,1)S(1)}, bf16[1536,384]{1,0:T(8,128)(2,1)}, u32[]{:S(2)}, u32[]{:S(2)}) collective-permute-start(bf16[1536,384]{1,0:T(8,128)(2,1)S(1)} %maximum_select_fusion.1), channel_id=1, source_target_pairs={{0,2},{2,0},{4,6},{6,4},{8,10},{10,8},{12,14},{14,12},{16,18},{18,... | collective-permute-start | bytes 3538952 | tf_op jit(solution)/shard_map/ppermute | solution.py:261
  (76 other events, 766.3 us)
Sparse Core Ops, SparseCore 0:
  21.6 57.7 all-gather.2

commit v2 on v1

v2 whole, which is shorter than its diff:
```python
import functools, math
import jax
import jax.numpy as jnp
from jax import lax
from jax.experimental import pallas as pl
from jax.experimental.pallas import tpu as pltpu
from jax.sharding import PartitionSpec as P

HEAD = 64
DEPTH = 12
EPSILON = 1e-05
BRANCH = 1.0 / math.sqrt(DEPTH)
GELU_C = math.sqrt(2.0 / math.pi)
SWAP = ((0, 1), (1, 0))
LOG2E = math.log2(math.e)
NT = (((1,), (1,)), ((), ()))
TN = (((0,), (0,)), ((), ()))
f32 = jnp.float32
bf16 = jnp.bfloat16


def attn_forward_kernel(blk, info, own_ref, oth_ref, w_ref, b_ref, qkv_ref, att_ref, lse_ref, acc_ref, top_ref):
    qb = pl.program_id(0)
    nb = pl.num_programs(0)
    half = own_ref.shape[0]
    width = w_ref.shape[2]
    side, count = info[0], info[1]

    @pl.when(qb == 0)
    def _():
        step = 256
        for part, ref in enumerate((own_ref, oth_ref)):
            def rows_loop(i, _, part=part, ref=ref):
                rows = ref[pl.ds(pl.multiple_of(i * step, step), step), :]
                to = pl.multiple_of(part * half + i * step, step)
                for j in range(3):
                    y = jnp.dot(rows, w_ref[j], preferred_element_type=f32) + b_ref[pl.ds(j, 1), :]
                    y = y.astype(bf16)
                    if j == 0:
                        y = y * bf16(0.125)
                    qkv_ref[pl.ds(to, step), pl.ds(j * width, width)] = y
                return 0
            lax.fori_loop(0, half // step, rows_loop, 0)

    def place(b):
        return pl.multiple_of(lax.rem(b + side * (nb // 2), nb) * blk, blk)

    lane_lo = lax.broadcasted_iota(jnp.int32, (blk, 128), 1) < HEAD
    first = (qb * count // nb) * nb // count
    q_at = place(qb)

    def block(kb, fresh, masked):
        k_at = place(kb)
        if masked:
            qi = lax.broadcasted_iota(jnp.int32, (blk, blk), 0)
            ki = lax.broadcasted_iota(jnp.int32, (blk, blk), 1)
            keep = ki <= qi
        for p in range(width // 128):
            q = qkv_ref[pl.ds(q_at, blk), pl.ds(0 * width + 128 * p, 128)]
            k = qkv_ref[pl.ds(k_at, blk), pl.ds(1 * width + 128 * p, 128)]
            v = qkv_ref[pl.ds(k_at, blk), pl.ds(2 * width + 128 * p, 128)]
            for h in range(2):
                mine = lane_lo if h == 0 else ~lane_lo
                head = 2 * p + h
                qh = jnp.where(mine, q, bf16(0))
                vh = jnp.where(mine, v, bf16(1))
                s = lax.dot_general(qh, k, NT, preferred_element_type=f32) * LOG2E
                if masked:
                    s = jnp.where(keep, s, -1e30)
                top = jnp.max(s, axis=1, keepdims=True)
                if fresh:
                    e = jnp.exp2(s - top)
                    acc_ref[head] = jnp.dot(e.astype(bf16), vh, preferred_element_type=f32)
                    top_ref[head] = jnp.broadcast_to(top, (blk, 128))
                else:
                    old = top_ref[head]
                    new = jnp.maximum(old, top)
                    e = jnp.exp2(s - new[:, :1])
                    acc_ref[head] = acc_ref[head] * jnp.exp2(old - new) + jnp.dot(
                        e.astype(bf16), vh, preferred_element_type=f32)
                    top_ref[head] = new

    block(qb, True, True)

    def loop(kb, _):
        block(kb, False, False)
        return 0
    lax.fori_loop(first, qb, loop, 0)

    for p in range(width // 128):
        a0, a1 = acc_ref[2 * p], acc_ref[2 * p + 1]
        num = jnp.where(lane_lo, a0, a1)
        den = jnp.where(lane_lo, pltpu.roll(a0, HEAD, 1), pltpu.roll(a1, HEAD, 1))
        att_ref[pl.ds(q_at, blk), pl.ds(128 * p, 128)] = (num / den).astype(bf16)
        logs = jnp.where(lane_lo, top_ref[2 * p], top_ref[2 * p + 1]) + jnp.log2(den)
        rows = logs.T
        lse_ref[qb, pl.ds(2 * p, 1), :] = rows[0:1]
        lse_ref[qb, pl.ds(2 * p + 1, 1), :] = rows[HEAD:HEAD + 1]


def attn_forward(info, own, oth, w, b, blk=512):
    half = own.shape[0]
    rows = 2 * half
    width = w.shape[2]
    nb = rows // blk
    heads = width // HEAD
    vm = pl.BlockSpec(memory_space=pltpu.VMEM)
    return pl.pallas_call(
        functools.partial(attn_forward_kernel, blk),
        grid=(nb,),
        in_specs=[pl.BlockSpec(memory_space=pltpu.SMEM), vm, vm, vm, vm],
        out_specs=[vm, vm, vm],
        out_shape=[jax.ShapeDtypeStruct((rows, 3 * width), bf16),
                   jax.ShapeDtypeStruct((rows, width), bf16),
                   jax.ShapeDtypeStruct((nb, 8, blk), f32)],
        scratch_shapes=[pltpu.VMEM((heads, blk, 128), f32), pltpu.VMEM((heads, blk, 128), f32)],
        compiler_params=pltpu.CompilerParams(vmem_limit_bytes=56 << 20),
        cost_estimate=pl.CostEstimate(flops=12_000_000_000, transcendentals=0, bytes_accessed=12_000_000),
        name="attn_forward",
    )(info, own, oth, w, b)


def ring_reduce_ticks(n, parts, local, refs, spot, dest):
    mate, slot, first, yin, fin, s_send, s_recv, a_send, a_recv, m_send, m_recv, y_sem = refs
    core, pos = spot["core"], spot["pos"]

    def put(src, dst, send, recv, to):
        return pltpu.make_async_remote_copy(src_ref=src, dst_ref=dst, send_sem=send, recv_sem=recv,
                                            device_id=dest[to], device_id_type=pl.DeviceIdType.MESH)

    def at(c):
        return lax.rem(c + 2 * n, n)

    def ring_copy(s):
        src = slot.at[jnp.maximum(s - 1, 0)]
        return put(src, slot.at[s], s_send.at[s], s_recv.at[s], "next")

    def gather_copy(s):
        c = core * n + at(pos + 1 - s)
        return put(fin.at[c], fin.at[c], a_send.at[s], a_recv.at[s], "next")

    def arrived(s):
        c = core * n + at(pos - s)
        return put(fin.at[c], fin.at[c], a_send.at[s], a_recv.at[s], "next")

    def mate_copy(s):
        c = core * n + at(pos + 1 - s)
        return put(fin.at[c], fin.at[c], m_send.at[s], m_recv.at[s], "mate")

    def mate_arrived(s):
        return put(fin.at[0], fin.at[0], m_send.at[s], m_recv.at[s], "mate")

    first_copy = put(first, slot.at[0], s_send.at[0], s_recv.at[0], "next")
    if parts == 2:
        y_copy = put(slot.at[n - 2, 1], yin, y_sem.at[0], y_sem.at[1], "peer")

    def tick(k):
        @pl.when(k == 0)
        def _():
            for part in range(parts):
                first[part] = (local(part, at(pos)).astype(f32) + mate[part, at(pos)].astype(f32)).astype(bf16)
            first_copy.start()

        @pl.when((k > 0) & (k < n))
        def _():
            s = k - 1
            put(slot.at[s], slot.at[s], s_send.at[s], s_recv.at[s], "next").wait_recv()
            c = at(pos - k)
            for part in range(parts):
                slot[s, part] = (slot[s, part].astype(f32) + local(part, c).astype(f32)
                                 + mate[part, c].astype(f32)).astype(bf16)

            @pl.when(k < n - 1)
            def _():
                ring_copy(k).start()
            if parts == 2:
                @pl.when(k == n - 1)
                def _():
                    y_copy.start()

        @pl.when(k == n)
        def _():
            if parts == 2:
                y_copy.wait_recv()
                fin[core * n + at(pos + 1)] = (slot[n - 2, 0].astype(f32) + yin[...].astype(f32)).astype(bf16)
            else:
                fin[core * n + at(pos + 1)] = slot[n - 2, 0]
            gather_copy(0).start()
            mate_copy(0).start()

        @pl.when(k > n)
        def _():
            s = k - n - 1
            arrived(s).wait_recv()

            @pl.when(s < n - 2)
            def _():
                gather_copy(s + 1).start()
            mate_copy(s + 1).start()

    def finish():
        first_copy.wait_send()

        def sends(s, _):
            ring_copy(s).wait_send()
            return 0
        lax.fori_loop(1, n - 1, sends, 0)
        if parts == 2:
            y_copy.wait_send()

        def gathers(s, _):
            gather_copy(s).wait_send()
            return 0
        lax.fori_loop(0, n - 1, gathers, 0)

        def mates(s, _):
            mate_copy(s).wait_send()
            mate_arrived(s).wait_recv()
            return 0
        lax.fori_loop(0, n, mates, 0)

    return tick, finish


def backward_kernel(size, blk, count_ref, qkv_hbm, att_ref, gown_hbm, goth_hbm, lse_ref, gw_hbm, own_ref, oth_ref,
                    w_hbm, gmix_hbm, small_ref, tok_ref, gain_ref, gm_ref,
                    fin_ref, tail_ref, gtok_ref, small_out, last_out,
                    qkv_ref, g_ref, delta_ref, dq_ref, dk_ref, dv_ref, w_ref,
                    gl_ref, mate_ref, slot_ref, first_ref, yin_ref,
                    t_ref, tmate_ref, tslot_ref, tfirst_ref,
                    da_ref, dsend_ref, drecv_ref, vb_ref, rb_ref, ub_ref, qb_ref, hb_ref,
                    in_sem, c_sem, s_send, s_recv, a_send, a_recv, m_send, m_recv, y_sem,
                    tc_sem, ts_send, ts_recv, ta_send, ta_recv, tm_send, tm_recv,
                    d_send, d_recv, v_send, v_recv, u_send, u_recv):
    n = size // 2
    bits = size.bit_length() - 1
    rows, total = qkv_ref.shape
    half = rows // 2
    width = total // 3
    dim = own_ref.shape[1]
    nb = rows // blk
    me, side = lax.axis_index("dp"), lax.axis_index("tensor")
    core, chip = lax.rem(me, 2), me // 2
    odd = lax.rem(chip, 2)
    p = (1 - odd) * (chip // 2) + odd * (n - 1 - chip // 2)

    def chip_at(q):
        up = q // (n // 2)
        return (1 - up) * 2 * q + up * (2 * (n - 1 - q) + 1)
    pos = (1 - core) * p + core * lax.rem(n - p, n)
    step = 1 - 2 * core
    dest = {
        "next": {"dp": 2 * chip_at(lax.rem(p + step + n, n)) + core},
        "prev": {"dp": 2 * chip_at(lax.rem(p - step + n, n)) + core},
        "mate": {"dp": me + 1 - 2 * core},
        "peer": {"tensor": 1 - side},
    }
    for b in range(1, bits):
        dest[b] = {"dp": me + (1 - 2 * lax.rem(me // (1 << b), 2)) * (1 << b)}
    dest[0] = dest["mate"]
    dest[bits] = dest["peer"]

    def fetch(src, dst, i):
        copy = pltpu.make_async_copy(src, dst, in_sem.at[i])
        copy.start()
        return copy
    gl_copy = fetch(gw_hbm.at[core], gl_ref, 0)
    q_copy = fetch(qkv_hbm, qkv_ref, 1)
    g0_copy = fetch(gown_hbm, g_ref.at[pl.ds(0, half)], 2)
    g1_copy = fetch(goth_hbm, g_ref.at[pl.ds(half, half)], 3)
    w_copies = [fetch(w_hbm.at[j], w_ref.at[:, pl.ds(j * width, width)], 4 + j) for j in range(3)]
    ch2 = t_ref.shape[1]
    gx_copy = fetch(gmix_hbm, t_ref.at[pl.ds(3 * dim // ch2, dim // ch2)], 7)

    barrier = pltpu.get_barrier_semaphore()
    friends = ["next", "prev", "mate", "peer"] + list(range(1, bits))
    for to in friends:
        pl.semaphore_signal(barrier, inc=1, device_id=dest[to], device_id_type=pl.DeviceIdType.MESH)
    pl.semaphore_wait(barrier, len(friends))

    def put(src, dst, send, recv, to):
        return pltpu.make_async_remote_copy(src_ref=src, dst_ref=dst, send_sem=send, recv_sem=recv,
                                            device_id=dest[to], device_id_type=pl.DeviceIdType.MESH)
    core_copy = put(gw_hbm.at[1 - core], mate_ref, c_sem.at[0], c_sem.at[1], "mate")
    core_copy.start()
    vb_ref[0] = small_ref[...]

    spot = {"core": core, "pos": pos}
    tick, finish = ring_reduce_ticks(
        n, 2, lambda part, c: gl_ref[part, c],
        (mate_ref, slot_ref, first_ref, yin_ref, fin_ref, s_send, s_recv, a_send, a_recv, m_send, m_recv, y_sem),
        spot, dest)
    ttick, tfinish = ring_reduce_ticks(
        n, 1, lambda part, c: t_ref[core * n + c],
        (tmate_ref, tslot_ref, tfirst_ref, None, tail_ref, ts_send, ts_recv, ta_send, ta_recv, tm_send, tm_recv,
         y_sem),
        spot, dest)

    def small_copy(buf, inbox, send, recv, b):
        return put(buf.at[b], inbox.at[b], send.at[b], recv.at[b], b)

    def small_start(b):
        small_copy(vb_ref, rb_ref, v_send, v_recv, b).start()

    def small_end(b):
        small_copy(vb_ref, rb_ref, v_send, v_recv, b).wait()
        if b < bits:
            vb_ref[b + 1] = vb_ref[b] + rb_ref[b]

    small_start(0)
    q_copy.wait()
    g0_copy.wait()
    g1_copy.wait()
    dq_ref[...] = jnp.zeros_like(dq_ref)
    hb_ref[...] = jnp.zeros_like(hb_ref)

    def place(b):
        return pl.multiple_of(lax.rem(b + side * (nb // 2), nb) * blk, blk)
    pick = (lax.broadcasted_iota(jnp.int32, (8, width), 1) // HEAD
            == lax.broadcasted_iota(jnp.int32, (8, width), 0)).astype(bf16)

    def deltas(b, _):
        spot_b = place(b)
        prod = g_ref[pl.ds(spot_b, blk), :].astype(f32) * att_ref[pl.ds(spot_b, blk), :].astype(f32)
        high = prod.astype(bf16)
        low = (prod - high.astype(f32)).astype(bf16)
        delta_ref[b] = (lax.dot_general(pick, high, NT, preferred_element_type=f32)
                        + lax.dot_general(pick, low, NT, preferred_element_type=f32))
        return 0
    lax.fori_loop(0, nb, deltas, 0)

    lane_lo = lax.broadcasted_iota(jnp.int32, (blk, 128), 1) < HEAD
    count = count_ref[0]

    def block(kb, qb, masked):
        k_at, q_at = place(kb), place(qb)
        if masked:
            keep = (lax.broadcasted_iota(jnp.int32, (blk, blk), 0)
                    <= lax.broadcasted_iota(jnp.int32, (blk, blk), 1))
        else:
            apart = jnp.where(kb * count // nb == qb * count // nb, 0.0, 1e30)
        for pr in range(width // 128):
            cols = [pl.ds(j * width + 128 * pr, 128) for j in range(3)]
            q = qkv_ref[pl.ds(q_at, blk), cols[0]]
            g = g_ref[pl.ds(q_at, blk), cols[0]]
            k = qkv_ref[pl.ds(k_at, blk), cols[1]]
            v = qkv_ref[pl.ds(k_at, blk), cols[2]]
            dk = dv = dq = None
            for h in range(2):
                mine = lane_lo if h == 0 else ~lane_lo
                head = 2 * pr + h
                kh = jnp.where(mine, k, bf16(0))
                vh = jnp.where(mine, v, bf16(0))
                s = lax.dot_general(kh, q, NT, preferred_element_type=f32) * LOG2E
                lse = lse_ref[qb, pl.ds(head, 1), :]
                if not masked:
                    lse = lse + apart
                e = jnp.exp2(s - lse)
                if masked:
                    e = jnp.where(keep, e, 0.0)
                dp = lax.dot_general(vh, g, NT, preferred_element_type=f32)
                ds = (e * (dp - delta_ref[qb, pl.ds(head, 1), :])).astype(bf16)
                e = e.astype(bf16)
                dv1 = jnp.dot(e, jnp.where(mine, g, bf16(0)), preferred_element_type=f32)
                dk1 = jnp.dot(ds, jnp.where(mine, q, bf16(0)), preferred_element_type=f32)
                dq1 = lax.dot_general(ds, kh, TN, preferred_element_type=f32)
                dk, dv, dq = (dk1, dv1, dq1) if h == 0 else (dk + dk1, dv + dv1, dq + dq1)
            if masked:
                dk_ref[:, cols[0]] = dk
                dv_ref[:, cols[0]] = dv
            else:
                dk_ref[:, cols[0]] += dk
                dv_ref[:, cols[0]] += dv
            dq_ref[pl.ds(q_at, blk), cols[0]] += dq

    pairs = nb * (nb + 1) // 2
    early = n

    def ticks(lo, hi):
        def one(k, _):
            @pl.when(k == 0)
            def _():
                gl_copy.wait()
                core_copy.wait()
            tick(k)
            return 0
        lax.fori_loop(lo, hi, one, 0)

    def small_ticks(i):
        for b in range(bits + 1):
            @pl.when(i == b + 1)
            def _(b=b):
                small_end(b)
                if b < bits:
                    small_start(b + 1)

    def key_block(kb, i):
        small_ticks(i)
        ticks(i * early // pairs, (i + 1) * early // pairs)
        block(kb, kb, True)

        def other(qb, i):
            small_ticks(i)
            ticks(i * early // pairs, (i + 1) * early // pairs)
            block(kb, qb, False)
            return i + 1
        i = lax.fori_loop(kb + 1, nb, other, i + 1)
        k_at = place(kb)
        for j, part in ((0, dq_ref[pl.ds(k_at, blk), :] * 0.125), (1, dk_ref[...]), (2, dv_ref[...])):
            low = part.astype(bf16)
            qkv_ref[pl.ds(k_at, blk), pl.ds(j * width, width)] = low
            if j != 1:
                hb_ref[j // 2] += jnp.sum(low.astype(f32), axis=0, keepdims=True)
        return i
    done = lax.fori_loop(0, nb, key_block, 0)
    for b in range(bits + 1):
        if b + 1 >= pairs:
            small_end(b)
            if b < bits:
                small_start(b + 1)
    v, r = vb_ref[bits], rb_ref[bits]
    small_out[...] = v + jnp.concatenate([r[0:4], r[6:8], r[6:8]])

    for copy in w_copies:
        copy.wait()
    piece = half // 4

    def da_copy(i):
        return put(dsend_ref.at[i], drecv_ref.at[i], d_send.at[i], d_recv.at[i], "peer")

    def send_rows(i, _):
        gq = qkv_ref[pl.ds(pl.multiple_of(half + i * piece, piece), piece), :]
        dsend_ref[i] = lax.dot_general(gq, w_ref[...], NT, preferred_element_type=f32).astype(bf16)
        da_copy(i).start()
        return 0
    lax.fori_loop(0, 4, send_rows, 0)

    def head_grads(i, _):
        at = pl.ds(pl.multiple_of(i * 384, 384), 384)
        acc = (lax.dot_general(own_ref[:, at], qkv_ref[pl.ds(0, half), :], TN, preferred_element_type=f32)
               + lax.dot_general(oth_ref[:, at], qkv_ref[pl.ds(half, half), :], TN, preferred_element_type=f32))
        for j in range(3):
            cut = acc[:, j * width:(j + 1) * width].reshape(384 // ch2, ch2, width).astype(bf16)
            t_ref[pl.ds((j * dim + i * 384) // ch2, 384 // ch2)] = cut
        return 0
    lax.fori_loop(0, dim // 384, head_grads, 0)
    gx_copy.wait()
    tcore_copy = put(t_ref.at[pl.ds((1 - core) * n, n)], tmate_ref.at[0], tc_sem.at[0], tc_sem.at[1], "mate")
    tcore_copy.start()

    def own_rows(i, _):
        at = pl.ds(pl.multiple_of(i * piece, piece), piece)
        da_ref[at, :] = lax.dot_general(qkv_ref[at, :], w_ref[...], NT, preferred_element_type=f32)
        return 0
    lax.fori_loop(0, 4, own_rows, 0)
    tcore_copy.wait()

    def tail_ticks(lo, hi):
        def one(k, _):
            ttick(k)
            return 0
        lax.fori_loop(lo, hi, one, 0)

    sums = jnp.zeros((2, dim), f32)
    ub_ref[0] = jnp.zeros((8, dim), f32)
    for i in range(4):
        ticks(early + i * n // 4, early + (i + 1) * n // 4)
        tail_ticks(i * n // 4, (i + 1) * n // 4)
        da_copy(i).wait()

        def norm_rows(j, _, i=i):
            inner = piece // 4
            at = pl.ds(pl.multiple_of(i * piece + j * inner, inner), inner)
            x = tok_ref[at, :].astype(f32)
            x = x - jnp.mean(x, axis=-1, keepdims=True)
            inv = lax.rsqrt(jnp.mean(x * x, axis=-1, keepdims=True) + EPSILON)
            h = x * inv
            e = da_ref[at, :] + drecv_ref[i, pl.ds(pl.multiple_of(j * inner, inner), inner), :].astype(f32)
            eg = e * gain_ref[...]
            back = inv * (eg - jnp.mean(eg, axis=-1, keepdims=True)
                          - h * jnp.mean(eg * h, axis=-1, keepdims=True))
            gtok_ref[at, :] = (gm_ref[at, :] + back).astype(bf16)
            ub_ref[0, 0:1, :] += jnp.sum(e * h, axis=0, keepdims=True)
            ub_ref[0, 1:2, :] += jnp.sum(e, axis=0, keepdims=True)
            return 0
        lax.fori_loop(0, 4, norm_rows, 0)
    ub_ref[0, 2:3, pl.ds(0, width)] = hb_ref[0]
    ub_ref[0, 2:3, pl.ds(width, width)] = hb_ref[1]
    last_copies = []
    for b in range(bits + 1):
        copy = small_copy(ub_ref, qb_ref, u_send, u_recv, b)
        copy.start()
        tail_ticks(n + b * n // (bits + 1), n + (b + 1) * n // (bits + 1))
        copy.wait()
        if b < bits:
            ub_ref[b + 1] = ub_ref[b] + qb_ref[b]
    v, r = ub_ref[bits], qb_ref[bits]
    last_out[...] = jnp.concatenate([v[0:2] + r[0:2], v[2:8]])
    finish()
    tfinish()


def backward(size, count, qkv, att, gown, goth, lse, gw, a1, a1_other, w, gmix, small, tokens, gain, grad_middle,
             blk=512):
    rows, total = qkv.shape
    width = total // 3
    half, dim = tokens.shape
    nb = rows // blk
    n = size // 2
    bits = size.bit_length() - 1
    hidden = gw.shape[2]
    gw = gw.reshape(2, 2, n, hidden // n, dim)
    ch, ch2 = hidden // n, 4 * dim // (2 * n)
    gmix = gmix.reshape(dim // ch2, ch2, width)
    vm = pl.BlockSpec(memory_space=pltpu.VMEM)
    hb = pl.BlockSpec(memory_space=pl.ANY)
    sm = pl.BlockSpec(memory_space=pltpu.SMEM)
    V, S = pltpu.VMEM, pltpu.SemaphoreType.DMA
    return pl.pallas_call(
        functools.partial(backward_kernel, size, blk),
        in_specs=[sm, hb, vm, hb, hb, vm, hb, vm, vm, hb, hb, vm, vm, vm, vm],
        out_specs=[vm] * 5,
        out_shape=[jax.ShapeDtypeStruct((2 * n, ch, dim), bf16),
                   jax.ShapeDtypeStruct((2 * n, ch2, width), bf16),
                   jax.ShapeDtypeStruct((half, dim), bf16),
                   jax.ShapeDtypeStruct((8, dim), f32),
                   jax.ShapeDtypeStruct((8, dim), f32)],
        scratch_shapes=[
            V((rows, total), bf16), V((rows, width), bf16), V((nb, 8, blk), f32), V((rows, width), f32),
            V((blk, width), f32), V((blk, width), f32), V((dim, total), bf16),
            V((2, n, ch, dim), bf16), V((2, n, ch, dim), bf16), V((n - 1, 2, ch, dim), bf16), V((2, ch, dim), bf16),
            V((ch, dim), bf16),
            V((2 * n, ch2, width), bf16), V((1, n, ch2, width), bf16), V((n - 1, 1, ch2, width), bf16),
            V((1, ch2, width), bf16),
            V((half, dim), f32), V((4, half // 4, dim), bf16), V((4, half // 4, dim), bf16),
            V((bits + 1, 8, dim), f32), V((bits + 1, 8, dim), f32), V((bits + 1, 8, dim), f32),
            V((bits + 1, 8, dim), f32), V((2, 1, width), f32),
            S((8,)), S((2,)), S((n - 1,)), S((n - 1,)), S((n - 1,)), S((n - 1,)), S((n,)), S((n,)), S((2,)),
            S((2,)), S((n - 1,)), S((n - 1,)), S((n - 1,)), S((n - 1,)), S((n,)), S((n,)),
            S((4,)), S((4,)), S((bits + 1,)), S((bits + 1,)), S((bits + 1,)), S((bits + 1,))],
        compiler_params=pltpu.CompilerParams(collective_id=0, has_side_effects=True,
                                             vmem_limit_bytes=67_043_328),
        cost_estimate=pl.CostEstimate(flops=40_000_000_000, transcendentals=0, bytes_accessed=30_000_000),
        name="backward",
    )(count, qkv, att, gown, goth, lse, gw, a1, a1_other, w, gmix, small, tokens, gain, grad_middle)


def to_peer(v):
    return lax.ppermute(v, "tensor", SWAP)


def row_stats(v):
    centre = jnp.mean(v, axis=-1, keepdims=True)
    centred = v - centre
    inv = lax.rsqrt(jnp.mean(centred * centred, axis=-1, keepdims=True) + EPSILON)
    return centre, inv


def norm_back(e, gain, h, inv):
    eg = e * gain
    return inv * (eg - jnp.mean(eg, axis=-1, keepdims=True)
                  - h * jnp.mean(eg * h, axis=-1, keepdims=True))


def add16(a, b):
    return (a.astype(f32) + b.astype(f32)).astype(bf16)


def dot32(a, b):
    return jnp.dot(a, b, preferred_element_type=f32)


def dot_nt(a, b):
    return lax.dot_general(a, b, NT, preferred_element_type=f32)


def dot_tn(a, b):
    return lax.dot_general(a, b, TN, preferred_element_type=f32)


def xor_step(v, size, bit):
    return lax.ppermute(v, "dp", [(i, i ^ (1 << bit)) for i in range(size)])


def gelu_pair(v):
    t = jnp.tanh(GELU_C * (v + 0.044715 * v * v * v))
    return 0.5 * v * (1.0 + t), 0.5 * (1.0 + t) + 0.5 * v * (1.0 - t * t) * (
        GELU_C * (1.0 + 3.0 * 0.044715 * v * v))


def local(
    tokens,
    seq_count,
    first_gain,
    first_shift,
    heads_weight,
    heads_bias,
    mixing_weight,
    mixing_bias,
    second_gain,
    second_shift,
    up_weight,
    up_bias,
    down_weight,
    down_bias,
    cotangent,
):
    size = lax.axis_size("dp")
    me = lax.axis_index("dp")
    side = lax.axis_index("tensor")
    info = jnp.stack([side.astype(jnp.int32), seq_count[0]])
    half, dim = tokens.shape
    width = heads_weight.shape[2]
    hidden = up_weight.shape[1]

    pu, pd, pm = dim // size, hidden // size, width // size
    piece = jnp.concatenate([
        lax.dynamic_slice(up_weight, (me * pu, 0), (pu, hidden // 2)),
        lax.dynamic_slice(up_weight, (me * pu, hidden // 2), (pu, hidden // 2)),
        lax.dynamic_slice_in_dim(down_weight, me * pd, pd, 0),
        lax.dynamic_slice_in_dim(mixing_weight, me * pm, pm, 0)])
    piece = to_peer(piece)
    up_bias_other = to_peer(up_bias)

    x = tokens.astype(f32)
    centre1, inv1 = row_stats(x)
    a1 = ((x - centre1) * inv1 * first_gain + first_shift).astype(bf16)
    piece, a1 = lax.optimization_barrier((piece, a1))
    a1_other = to_peer(a1)
    packed = lax.all_gather(piece, "dp", axis=0)
    up_other = jnp.concatenate([packed[:, :pu].reshape(dim, hidden // 2),
                                packed[:, pu:2 * pu].reshape(dim, hidden // 2)], axis=1)
    down_other = packed[:, 2 * pu:2 * pu + pd].reshape(hidden, dim)
    mix_other = packed[:, 2 * pu + pd:].reshape(width, dim)
    bias3 = jnp.stack([heads_bias[0], jnp.zeros_like(heads_bias[0]), heads_bias[1]])
    qkv, att, lse = attn_forward(info, a1, a1_other, heads_weight, bias3)
    att_mine = att[:half]
    att_recv = to_peer(att[half:])
    middle = x + BRANCH * (dot32(att_mine, mixing_weight) + dot32(att_recv, mix_other) + mixing_bias)
    centre2, inv2 = row_stats(middle)
    h2 = (middle - centre2) * inv2
    a2 = (h2 * second_gain + second_shift).astype(bf16)

    g_out = cotangent.astype(f32)
    grad_mlp = (BRANCH * g_out).astype(bf16)
    down_sum = 0.0
    grad_a2 = 0.0
    grads_up, grads_down, bias_up = [], [], []
    for up, bias, down in ((up_weight, up_bias, down_weight), (up_other, up_bias_other, down_other)):
        pre = dot32(a2, up) + bias
        act, slope = gelu_pair(pre)
        act = act.astype(bf16)
        down_sum += dot32(act, down)
        grad_pre = (dot_nt(grad_mlp, down) * slope).astype(bf16)
        grads_down.append(dot_tn(act, grad_mlp).astype(bf16))
        grads_up.append(jnp.concatenate([dot_tn(a2, grad_pre[:, :hidden // 2]),
                                         dot_tn(a2, grad_pre[:, hidden // 2:])]).astype(bf16))
        bias_up.append(jnp.sum(grad_pre, axis=0, dtype=f32).reshape(2, dim))
        grad_a2 += dot_nt(grad_pre, up)
    result = (middle + BRANCH * (down_sum + down_bias)).astype(bf16)
    grads = jnp.stack([jnp.stack(grads_down), jnp.stack(grads_up)])

    grad_middle = g_out + norm_back(grad_a2, second_gain, h2, inv2)
    grad_attn = (BRANCH * grad_middle).astype(bf16)
    g_own = dot_nt(grad_attn, mixing_weight).astype(bf16)
    g_other = to_peer(dot_nt(grad_attn, mix_other).astype(bf16))
    small = jnp.concatenate([
        jnp.stack([BRANCH * jnp.sum(g_out, axis=0), jnp.sum(grad_a2 * h2, axis=0),
                   jnp.sum(grad_a2, axis=0), BRANCH * jnp.sum(grad_middle, axis=0)])] + bias_up)
    grad_mix = add16(dot_tn(att_mine, grad_attn), to_peer(dot_tn(att_recv, grad_attn).astype(bf16)))

    grad_mix = jnp.concatenate([grad_mix[:, :width], grad_mix[:, width:]])
    fin, tail, grad_tokens, small, last = backward(
        size, seq_count, qkv, att, g_own, g_other, lse, grads, a1, a1_other, heads_weight, grad_mix, small,
        tokens, first_gain[None], grad_middle)
    groups = 1.0 / size
    small = small * groups
    last = last * groups
    fin = fin.reshape(2, hidden, dim).astype(f32) * groups
    tail = tail.reshape(4 * dim, width).astype(f32) * groups
    grad_up = fin[1]
    return (
        result,
        grad_tokens,
        last[0],
        last[1],
        tail[:3 * dim].reshape(3, dim, width),
        last[2].reshape(2, width),
        jnp.concatenate([tail[3 * dim:3 * dim + width], tail[3 * dim + width:]], axis=1),
        small[3],
        small[1],
        small[2],
        jnp.concatenate([grad_up[:dim], grad_up[dim:]], axis=1),
        small[4:6].reshape(hidden),
        fin[0],
        small[0],
    )


def solution(mesh):
    placed = (
        P(("dp", "tensor"), None),
        P("dp"),
        P(),
        P(),
        P(None, None, "tensor"),
        P(None, "tensor"),
        P("tensor", None),
        P(),
        P(),
        P(),
        P(None, "tensor"),
        P("tensor"),
        P("tensor", None),
        P(),
        P(("dp", "tensor"), None),
    )
    return jax.shard_map(
        local,
        mesh=mesh,
        in_specs=placed,
        out_specs=(
            P(("dp", "tensor"), None),
            P(("dp", "tensor"), None),
            P(),
            P(),
            P(None, None, "tensor"),
            P(None, "tensor"),
            P("tensor", None),
            P(),
            P(),
            P(),
            P(None, "tensor"),
            P("tensor"),
            P("tensor", None),
            P(),
        ),
        check_vma=False,
    )
```

time: 478 us -> 430 us (0.90)
  Pallas kernels: 99.4 us -> 244 us
  waiting for transfers between devices: 158 us -> 43.2 us
  matrix products: 86 us -> 61.3 us
  starting transfers between devices: 32.2 us -> 9.02 us
  other arithmetic: 37.5 us -> 22.4 us
  between operations: 27 us -> 15.7 us
    pallas_call x1, Pallas kernels: 53.3 us -> 198 us  [backward(): pl.pallas_call(functools.partial(backward_kernel, size, blk), in_specs=[s...]
    ppermute x32 -> x0, waiting for transfers between devices: 103 us -> none  [the longest x7 49.5 us: ring_reduce(): moving = add16(lax.ppermute(moving, 'dp', pairs), chunk(pos - s - 1))]
    dot_general x14 -> x8, matrix products: 37.9 us -> 16.6 us  [dot_tn(): return lax.dot_general(a, b, TN, preferred_element_type=f32)]
    ppermute x32 -> x0, starting transfers between devices: 17.3 us -> none  [the longest x18 14.1 us: xor_step(): return lax.ppermute(v, 'dp', [(i, i ^ 1 << bit) for i in range(size)])]
    ppermute x10 -> x6, waiting for transfers between devices: 55 us -> 43.2 us  [to_peer(): return lax.ppermute(v, 'tensor', SWAP)]
    convert_element_type x13 -> x0, other arithmetic: 7.9 us -> none  [the longest x12 5.71 us: add16(): return (a.astype(f32) + b.astype(f32)).astype(bf16)]
    ppermute x10 -> x6, starting transfers between devices: 14.9 us -> 8.98 us  [to_peer(): return lax.ppermute(v, 'tensor', SWAP)]
    dynamic_update_slice x7 -> x0, local copies, waits for them, and re-layouts: 5.13 us -> none  [ring_reduce(): lax.dynamic_update_index_in_dim(full, done, lax.rem(pos - s + chips, chip...]
  transfers between devices with their start and end apart: 43 -> 7, of which waited for: 25 -> 3; matrix products, arithmetic and copies ran while one was open for 24% -> 11% of each run, Pallas kernels for 21% -> 11%
where the time goes in v2:
time: 430 us; the launch traced here: 423 us
  Pallas kernels  244 us (57%)
  matrix products  61.3 us (14%)
  waiting for transfers between devices  43.2 us (10%)
  local copies, waits for them, and re-layouts  26.9 us (6%)
  other arithmetic  22.4 us (5%)
  between operations  15.7 us (4%)
  starting transfers between devices  9.02 us (2%)
    pallas_call x1, Pallas kernels, backward(): pl.pallas_call(functools.partial(backward_kernel, size, blk), in_specs=[s...  198 us
    pallas_call x1, Pallas kernels, attn_forward(): pl.pallas_call(functools.partial(attn_forward_kernel, blk), grid=(nb,), i...  45.9 us
    ppermute x6, waiting for transfers between devices, to_peer(): return lax.ppermute(v, 'tensor', SWAP)  43.2 us
    dot_general x6, matrix products, dot_nt(): return lax.dot_general(a, b, NT, preferred_element_type=f32)  24.4 us
    dot_general x6, matrix products, dot32(): return jnp.dot(a, b, preferred_element_type=f32)  20.3 us
    dot_general x8, matrix products, dot_tn(): return lax.dot_general(a, b, TN, preferred_element_type=f32)  16.6 us
    ppermute x6, starting transfers between devices, to_peer(): return lax.ppermute(v, 'tensor', SWAP)  8.98 us
  transfers between devices with their start and end apart: 7, of which 3 were waited for; matrix products, arithmetic and copies ran while one was open for 11% of the time, Pallas kernels for 11%

profile of v2, /device:TPU:0, one launch (start us, length us, event | category | flops | bytes accessed | tf_op | source)
XLA Modules:
  0.0 422.6 jit_solution(6866895921829911356)
XLA Ops:
  10.1 3.1 collective-permute-start
  16.1 4.8 %collective-permute-done = bf16[216,768]{1,0:T(8,128)(2,1)S(1)} collective-permute-done((bf16[216,768]{1,0:T(8,128)(2,1)S(1)}, bf16[216,768]{1,0:T(8,128)(2,1)S(1)}, u32[]{:S(2)}, u32[]{:S(2)}) %collective-permute-start) | collective-permute-done | bytes 331808 | tf_op jit(solution)/shard_map/ppermute | solution.py:549
  25.5 31.9 %collective-permute-done.1.oth_ref = bf16[1024,768]{1,0:T(8,128)(2,1)} collective-permute-done((bf16[1024,768]{1,0:T(8,128)(2,1)S(1)}, bf16[1024,768]{1,0:T(8,128)(2,1)}, u32[]{:S(2)}, u32[]{:S(2)}) %collective-permute-start.1) | collective-permute-done | bytes 1572896 | tf_op jit(solution)/shard_map/ppermute | solution.py:549
  57.4 45.9 %attn_forward.1 = (bf16[2048,1152]{1,0:T(8,128)(2,1)}, bf16[2048,384]{1,0:T(8,128)(2,1)}, f32[4,8,512]{2,1,0:T(8,128)}) custom-call(s32[2]{0:T(128)} %pad_add_fusion.info, bf16[1024,768]{1,0:T(8,128)(2,1)} %copy-done.3, bf16[1024,768]{1,0:T(8,128)(2,1)} %collective-permute-done.1.oth_ref, bf16[3,768,384]{2,1,0:T(8,128)(2,1)} %w_hbm.1, ...), custom_call_target="tpu_custom_call" | custom-call | flops 12000000000 | bytes 12000000 | tf_op jit(solution)/shard_map/attn_forward/pallas_call | solution.py:108
  110.1 6.4 %collective-permute-done.2 = bf16[1024,384]{1,0:T(8,128)(2,1)S(1)} collective-permute-done((bf16[1024,384]{1,0:T(8,128)(2,1)S(1)}, bf16[1024,384]{1,0:T(8,128)(2,1)S(1)}, u32[]{:S(2)}, u32[]{:S(2)}) %collective-permute-start.2) | collective-permute-done | bytes 786464 | tf_op jit(solution)/shard_map/ppermute | solution.py:549
  121.1 6.0 %multiply_convert_fusion.1 = (bf16[1024,1536]{1,0:T(8,128)(2,1)}, f32[1024,1536]{1,0:T(8,128)}) fusion(f32[1536]{0:T(1024)S(1)} %copy-done.20, bf16[1024,768]{1,0:T(8,128)(2,1)S(1)} %add_convert_fusion.1, bf16[768,1536]{1,0:T(8,128)(2,1)S(1)} %copy-done.14), kind=kOutput, calls=%fused_computation.25 | convolution fusion | flops 2431647744 | bytes 13375488 | tf_op jit(solution)/shard_map/dot_general | solution.py:570
  127.1 2.6 fusion.43
  129.7 3.7 slice.136
  134.1 6.1 %convert_reduce_fusion = (f32[1536]{0:T(1024)S(1)}, bf16[1024,1536]{1,0:T(8,128)(2,1)S(1)}) fusion(f32[1024,1536]{1,0:T(8,128)S(1)} %fusion.43, f32[1536]{0:T(1024)S(1)} %collective-permute-done.3, bf16[1536,768]{1,0:T(8,128)(2,1)S(1)} %bitcast.67, bf16[1024,768]{1,0:T(8,128)(2,1)S(1)} %copy-done.5), kind=kOutput, calls=%fused_computation.22 | convolution fusion | flops 2452879872 | bytes 13381632 | tf_op jit(solution)/shard_map/dot_general | solution.py:574
  143.3 8.3 %convert_reduce_fusion.1 = (f32[1536]{0:T(1024)S(1)}, bf16[1024,1536]{1,0:T(8,128)(2,1)S(1)}) fusion(f32[1024,1536]{1,0:T(8,128)} %get-tuple-element.63, f32[1536]{0:T(1024)S(1)} %copy-done.20, bf16[1536,768]{1,0:T(8,128)(2,1)S(1)} %copy-done.15, bf16[1024,768]{1,0:T(8,128)(2,1)S(1)} %copy-done.5), kind=kOutput, calls=%fused_computation.23 | convolution fusion | flops 2452879872 | bytes 13381632 | tf_op jit(solution)/shard_map/dot_general | solution.py:574
  151.6 2.6 fusion.77
  157.6 4.3 %fusion.76 = f32[1024,768]{1,0:T(8,128)} fusion(bf16[1024,1536]{1,0:T(8,128)(2,1)S(1)} %copy-done.24, bf16[1536,768]{1,0:T(8,128)(2,1)S(1)} %copy-done.15), kind=kOutput, calls=%fused_computation.120 | convolution fusion | flops 2415919104 | bytes 8650752 | tf_op jit(solution)/shard_map/dot_general | solution.py:570
  161.9 2.9 convolution_convert_fusion.1
  164.8 3.6 multiply_reduce_fusion
  177.3 4.2 %convolution_convert_fusion = bf16[1536,768]{1,0:T(8,128)(2,1)S(1)} fusion(bf16[1024,768]{1,0:T(8,128)(2,1)S(1)} %copy-done.5, f32[1024,1536]{1,0:T(8,128)S(1)} %bitcast.77, f32[1536]{0:T(1024)S(1)} %collective-permute-done.3), kind=kOutput, calls=%fused_computation.36 | convolution fusion | flops 2435186688 | bytes 10229760 | tf_op jit(solution)/shard_map/dot_general | solution.py:578
  181.6 4.5 %maximum_maximum_fusion.gw_hbm = bf16[2,2,8,192,768]{4,3,2,1,0:T(8,128)(2,1)} fusion(bf16[1,1,8,192,768]{4,3,2,1,0:T(8,128)(2,1)S(1)} %bitcast.56, bf16[1,1,8,192,768]{4,3,2,1,0:T(8,128)(2,1)S(1)} %bitcast.57, bf16[1,1,8,192,768]{4,3,2,1,0:T(8,128)(2,1)S(1)} %bitcast.64, bf16[1,1,8,192,768]{4,3,2,1,0:T(8,128)(2,1)S(1)} %bitcast.63), kind=kLoop, calls=%fused_computation.4 | loop fusion | flops 14155776 | bytes 18874368 | tf_op jit(solution)/shard_map/stack | solution.py:661
  186.1 5.2 %add_convert_fusion = bf16[1024,768]{1,0:T(8,128)(2,1)} fusion(f32[1024,768]{1,0:T(8,128)S(1)} %get-tuple-element.61, f32[1024,768]{1,0:T(8,128)S(1)} %copy-done.23, bf16[1536,768]{1,0:T(8,128)(2,1)S(1)} %bitcast.68, f32[768]{0:T(1024)S(1)} %copy-done.21, f32[1024,1536]{1,0:T(8,128)S(1)} %bitcast.77, f32[1536]{0:T(1024)S(1)} %collective-permute-done.3), kind=kOutput, calls=%fused_computation.46 | convolution fusion | flops 2435579904 | bytes 16524288 | tf_op jit(solution)/shard_map/dot_general | solution.py:570
  191.4 1.9 convolution_convert_fusion.3.gown_hbm
  196.8 198.2 %backward.1 = (bf16[16,192,768]{2,1,0:T(8,128)(2,1)}, bf16[16,192,384]{2,1,0:T(8,128)(2,1)}, bf16[1024,768]{1,0:T(8,128)(2,1)}, f32[8,768]{1,0:T(8,128)}, f32[8,768]{1,0:T(8,128)}) custom-call(s32[1]{0:T(128)S(6)} %copy.34.count_ref, bf16[2048,1152]{1,0:T(8,128)(2,1)} %get-tuple-element.27.qkv_hbm, bf16[2048,384]{1,0:T(8,128)(2,1)} %get-tuple-element.25.att_ref, ...), custom_call_target="tpu_custom_call" | custom-call | flops 40000000000 | bytes 30000000 | tf_op jit(solution)/shard_map/backward/pallas_call | solution.py:519
  395.0 2.1 convert_multiply_fusion.2
  397.1 2.0 slice.145
  401.1 3.2 convert_multiply_fusion
  404.4 2.5 slice.155
  411.3 2.9 pad_maximum_fusion
  (123 shorter events, 47.8 us)
Async XLA Ops:
  7.2 7.6 %copy-start = (bf16[1024,768]{1,0:T(8,128)(2,1)S(1)}, bf16[1024,768]{1,0:T(8,128)(2,1)}, u32[]{:S(2)}) copy-start(bf16[1024,768]{1,0:T(8,128)(2,1)} %tok_ref.1) | copy-start | bytes 4718596
  7.2 8.2 %copy-start.16 = (f32[768]{0:T(1024)S(1)}, f32[768]{0:T(1024)}, u32[]{:S(2)}) copy-start(f32[768]{0:T(1024)} %param.18) | copy-start | bytes 9220
  7.2 8.2 %copy-start.13 = (f32[768]{0:T(1024)S(1)}, f32[768]{0:T(1024)}, u32[]{:S(2)}) copy-start(f32[768]{0:T(1024)} %param.17) | copy-start | bytes 9220
  7.2 100.0 %all-gather.3.cloned.1.call-start = ((), (), s32[]{:S(2)}) async-start(), calls=%async_computation | async-start | bytes 5640192 | tf_op jit(solution)/shard_map/all_gather | solution.py:630
  10.0 14.7 %copy-start.19 = (f32[2,384]{1,0:T(2,128)S(1)}, f32[2,384]{1,0:T(2,128)}, u32[]{:S(2)}) copy-start(f32[2,384]{1,0:T(2,128)} %param.20) | copy-start | bytes 9220
  10.1 10.9 %collective-permute-start = (bf16[216,768]{1,0:T(8,128)(2,1)S(1)}, bf16[216,768]{1,0:T(8,128)(2,1)S(1)}, u32[]{:S(2)}, u32[]{:S(2)}) collective-permute-start(bf16[216,768]{1,0:T(8,128)(2,1)S(1)} %pad_maximum_fusion.8), channel_id=1, source_target_pairs={{0,1},{1,0},{2,3},{3,2},{4,5},{5,4},{6,7},{7,6},{8,9},{9,8},{10,11... | collective-permute-start | bytes 995336 | tf_op jit(solution)/shard_map/ppermute | solution.py:549
  16.1 41.3 %copy-start.3 = (bf16[1024,768]{1,0:T(8,128)(2,1)}, bf16[1024,768]{1,0:T(8,128)(2,1)S(1)}, u32[]{:S(2)}) copy-start(bf16[1024,768]{1,0:T(8,128)(2,1)S(1)} %fusion.21.own_ref) | copy-start | bytes 4718596
  21.7 35.7 %collective-permute-start.1 = (bf16[1024,768]{1,0:T(8,128)(2,1)S(1)}, bf16[1024,768]{1,0:T(8,128)(2,1)}, u32[]{:S(2)}, u32[]{:S(2)}) collective-permute-start(bf16[1024,768]{1,0:T(8,128)(2,1)S(1)} %fusion.21.own_ref), channel_id=1, source_target_pairs={{0,1},{1,0},{2,3},{3,2},{4,5},{5,4},{6,7},{7,6},{8,9},{9,8},{10,11... | collective-permute-start | bytes 4718600 | tf_op jit(solution)/shard_map/ppermute | solution.py:549
  25.5 80.6 %copy-start.20 = (f32[1536]{0:T(1024)S(1)}, f32[1536]{0:T(1024)}, u32[]{:S(2)}) copy-start(f32[1536]{0:T(1024)} %param.26) | copy-start | bytes 18436
  104.5 12.1 %collective-permute-start.2 = (bf16[1024,384]{1,0:T(8,128)(2,1)S(1)}, bf16[1024,384]{1,0:T(8,128)(2,1)S(1)}, u32[]{:S(2)}, u32[]{:S(2)}) collective-permute-start(bf16[1024,384]{1,0:T(8,128)(2,1)S(1)} %slice.104), channel_id=1, source_target_pairs={{0,1},{1,0},{2,3},{3,2},{4,5},{5,4},{6,7},{7,6},{8,9},{9,8},{10,11... | collective-permute-start | bytes 2359304 | tf_op jit(solution)/shard_map/ppermute | solution.py:549
  106.0 27.4 %collective-permute-start.3 = (f32[1536]{0:T(1024)S(1)}, f32[1536]{0:T(1024)S(1)}, u32[]{:S(2)}, u32[]{:S(2)}) collective-permute-start(f32[1536]{0:T(1024)S(1)} %copy-done.20), channel_id=1, source_target_pairs={{0,1},{1,0},{2,3},{3,2},{4,5},{5,4},{6,7},{7,6},{8,9},{9,8},{10,11... | collective-permute-start | bytes 18440 | tf_op jit(solution)/shard_map/ppermute | solution.py:549
  110.1 7.5 %copy-start.6 = (bf16[2048,384]{1,0:T(8,128)(2,1)S(1)}, bf16[2048,384]{1,0:T(8,128)(2,1)}, u32[]{:S(2)}) copy-start(bf16[2048,384]{1,0:T(8,128)(2,1)} %get-tuple-element.25.att_ref) | copy-start | bytes 4718596
  110.1 7.5 %copy-start.8 = (bf16[384,768]{1,0:T(8,128)(2,1)S(1)}, bf16[384,768]{1,0:T(8,128)(2,1)}, u32[]{:S(2)}) copy-start(bf16[384,768]{1,0:T(8,128)(2,1)} %param.21) | copy-start | bytes 1769476
  110.1 7.5 %copy-start.17 = (f32[768]{0:T(1024)S(1)}, f32[768]{0:T(1024)}, u32[]{:S(2)}) copy-start(f32[768]{0:T(1024)} %param.22) | copy-start | bytes 9220
  129.7 10.5 %copy-start.22 = (f32[1024,1536]{1,0:T(8,128)}, f32[1024,1536]{1,0:T(8,128)S(1)}, u32[]{:S(2)}) copy-start(f32[1024,1536]{1,0:T(8,128)S(1)} %fusion.43) | copy-start | bytes 18874372
  129.7 4.4 %copy-start.5 = (bf16[1024,768]{1,0:T(8,128)(2,1)S(1)}, bf16[1024,768]{1,0:T(8,128)(2,1)}, u32[]{:S(2)}) copy-start(bf16[1024,768]{1,0:T(8,128)(2,1)} %param.29) | copy-start | bytes 4718596
  172.5 24.3 %collective-permute-start.4 = (bf16[1024,384]{1,0:T(8,128)(2,1)}, bf16[1024,384]{1,0:T(8,128)(2,1)}, u32[]{:S(2)}, u32[]{:S(2)}) collective-permute-start(bf16[1024,384]{1,0:T(8,128)(2,1)} %convolution_convert_fusion.2), channel_id=1, source_target_pairs={{0,1},{1,0},{2,3},{3,2},{4,5},{5,4},{6,7},{7,6},{8,9},{9,8},{10,11... | collective-permute-start | bytes 2359304 | tf_op jit(solution)/shard_map/ppermute | solution.py:549
  173.9 2.5 slice-start
  175.6 18.4 %collective-permute-start.5 = (bf16[384,768]{1,0:T(8,128)(2,1)}, bf16[384,768]{1,0:T(8,128)(2,1)}, u32[]{:S(2)}, u32[]{:S(2)}) collective-permute-start(bf16[384,768]{1,0:T(8,128)(2,1)} %convolution_convert_fusion.4), channel_id=1, source_target_pairs={{0,1},{1,0},{2,3},{3,2},{4,5},{5,4},{6,7},{7,6},{8,9},{9,8},{10,11... | collective-permute-start | bytes 1769480 | tf_op jit(solution)/shard_map/ppermute | solution.py:549
  181.6 4.5 %copy-start.21 = (f32[768]{0:T(1024)S(1)}, f32[768]{0:T(1024)}, u32[]{:S(2)}) copy-start(f32[768]{0:T(1024)} %param.28) | copy-start | bytes 9220
  181.6 4.5 %copy-start.23 = (f32[1024,768]{1,0:T(8,128)S(1)}, f32[1024,768]{1,0:T(8,128)}, u32[]{:S(2)}) copy-start(f32[1024,768]{1,0:T(8,128)} %fusion.76) | copy-start | bytes 9437188
  191.4 2.6 copy-start.7
  397.1 2.8 copy-start.10
  411.3 2.9 copy-start.4
  (10 other events, 15.6 us)
Sparse Core Ops, SparseCore 0:
  21.8 57.7 all-gather.2
